TPU v7x, 256 devices: a whole 4x4x8 slice. The times are simulated.
256 devices in a mesh: seq: 64 (over x, z, core), head: 4 (over y).
Axes of the slice: x: 4, y: 4, z: 8, core: 2. Of those that a mesh axis runs over, the one named last changes fastest.
Arguments:
- queries: bfloat16 [16384, 64, 128], P('seq', 'head'), may hold values from -360 to 360
- head_weights: bfloat16 [16384, 64], P('seq', 'head'), may hold values from -0.75 to 0.75
- keys: bfloat16 [16384, 128], P('seq'), may hold values from -6 to 6
- targets: bfloat16 [16384, 2048], P('seq'), may hold values from 0.0099487305 to 10
- chosen: int32 [128, 16], P('seq'), may hold values from -1 to 127, as said below
- tile_block: int32 [128], replicated, may hold values from 0 to 127, as said below
Outputs:
- query_grads: bfloat16 [16384, 64, 128], P('seq', 'head')
- weight_grads: float32 [16384, 64], P('seq', 'head')
- key_grads: float32 [16384, 128], P('seq')
- loss: float32 [], replicated
Inputs may be any that keep to these rules, and one draw needn't show every extreme that they name: `tile_block`: a permutation of 0 to 127; each aligned group of 4 stored positions holds the global blocks of that same group. `chosen`: slot 0 of stored tile p is tile_block[p]; live entries of a row are distinct, none exceeds tile_block[p], and they precede the -1 entries; over all tiles of one device of seq, at most 1 distinct live block is stored on any one other device.
All inputs are finite; a program needn't handle non-finite values.
Results may differ from a plain program's by a relative error of at most 0.0095.
Values may be sent and summed in bfloat16 or wider, within the bound.
A program may use at most 128 MiB of HBM per device.

v0:
```python
import jax
import jax.numpy as jnp
from jax import lax
from jax.sharding import Mesh
from jax.sharding import PartitionSpec as P

BLOCK = 128
SLOTS = 16
CAP = 1
KEYS = 2048
SEQ = ("seq_0", "seq_1", "seq_2")
SEQ_HEAD = ("seq_0", "seq_1", "seq_2", "head")


loss_scale = 4194304.0


def over_axes(value, axes):
    for axis in axes:
        value = lax.psum(value, axis)
    return value


def copy_for_each(value, axis):
    copies = jnp.broadcast_to(value, (lax.axis_size(axis), *value.shape))
    return lax.all_to_all(copies, axis, split_axis=0, concat_axis=0, tiled=True)


def over_copies(value, axis):
    return copy_for_each(value, axis).astype(jnp.float32).sum(axis=0)


def row_statistics(score_part, mask_part, target_part):
    row_max = jnp.max(jnp.where(mask_part, score_part, -1e30), axis=1)
    exp_terms = jnp.where(
        mask_part, jnp.exp(jnp.where(mask_part, score_part - row_max[:, None], 0.0)), 0.0
    )
    return (row_max, jnp.sum(exp_terms, axis=1), jnp.sum(target_part, axis=1))


def local(queries, head_weights, keys, targets, chosen, tile_block):
    row_count, heads_here, key_width = queries.shape
    tiles_here = row_count // BLOCK
    block_count = tile_block.shape[0]
    owner_count = block_count // tiles_here
    score_scale = key_width ** (-0.5)
    seq_index = lax.axis_index(SEQ)
    head_index = lax.axis_index("head")
    is_first = (head_index == 0).astype(jnp.float32)
    positions = jnp.arange(block_count, dtype=jnp.int32)
    home_of = jnp.sum(
        jnp.where(tile_block[None, :] == positions[:, None], positions[None, :], 0), axis=1
    )
    live_slot = chosen >= 0
    position = home_of[jnp.maximum(chosen, 0)]
    owner_index = position // tiles_here
    local_slot = position % tiles_here
    own_block = lax.dynamic_slice_in_dim(tile_block, seq_index * tiles_here, tiles_here)
    offsets = jnp.arange(BLOCK, dtype=jnp.int32)
    causal = offsets[None, :] <= offsets[:, None]
    own_slot = chosen == own_block[:, None]
    live_mask = live_slot[:, None, :, None] & (
        (~own_slot)[:, None, :, None] | causal[None, :, None, :]
    )
    live_mask = live_mask.reshape(row_count, KEYS)
    key_blocks = keys.reshape(tiles_here, BLOCK, key_width)
    remote = live_slot & (owner_index != seq_index)
    remote_pos = jnp.where(remote, position, -1).reshape(-1)
    wanted = jnp.any(remote_pos[:, None] == positions[None, :], axis=0).reshape(
        owner_count, tiles_here
    )
    slot_rank = jnp.cumsum(wanted.astype(jnp.int32), axis=1) - 1
    local_iota = jnp.arange(tiles_here, dtype=jnp.int32)
    request = jnp.stack(
        [jnp.sum(jnp.where(wanted & (slot_rank == 0), local_iota[None, :], 0), axis=1)], axis=1
    )
    asked_slots = lax.all_to_all(request, SEQ, split_axis=0, concat_axis=0, tiled=True)
    reply_blocks = key_blocks[asked_slots]
    arrived = lax.all_to_all(reply_blocks, SEQ, split_axis=0, concat_axis=0, tiled=True)
    key_table = jnp.concatenate(
        [key_blocks, arrived.reshape(owner_count * CAP, BLOCK, key_width)], axis=0
    )
    table_index = jnp.where(
        owner_index == seq_index,
        local_slot,
        tiles_here + owner_index * CAP + slot_rank[owner_index, local_slot],
    )
    table_index = jnp.where(live_slot, table_index, 0)
    fetched = key_table[table_index]
    query_tiles = queries.reshape(tiles_here, BLOCK, heads_here, key_width)
    weight_tiles = head_weights.astype(jnp.float32).reshape(tiles_here, BLOCK, heads_here)

    def dot_values(query_tile, key_tile):
        return jnp.einsum(
            "qhd,kd->qhk",
            query_tile,
            key_tile.reshape(-1, key_width),
            preferred_element_type=jnp.float32,
        )

    def forward(operands):
        query_tile, weight_tile, key_tile = operands
        values = dot_values(query_tile, key_tile)
        return score_scale * jnp.sum(jnp.maximum(values, 0.0) * weight_tile[:, :, None], axis=1)

    partial_value = lax.map(forward, (query_tiles, weight_tiles, fetched)).reshape(row_count, KEYS)
    target_vals = jnp.where(live_mask, targets.astype(jnp.float32), 0.0)
    pair_local = jnp.sum(live_mask.astype(jnp.float32))
    score_part = lax.psum(partial_value, "head")
    row_max, row_norm, row_target = row_statistics(score_part, live_mask, target_vals)
    target_prob = jnp.where(live_mask, target_vals / row_target[:, None], 0.0)
    kl_cols = jnp.sum(
        jnp.where(
            live_mask,
            target_prob * (jnp.log(jnp.where(live_mask, target_prob, 1.0)) - score_part),
            0.0,
        )
    )
    lse_sum = jnp.sum(row_max + jnp.log(row_norm))
    loss_part = is_first * (kl_cols + lse_sum)
    loss_total, pair_count = (
        over_axes(loss_part, SEQ_HEAD),
        over_axes(is_first * pair_local, SEQ_HEAD),
    )
    softmax_vals = (
        jnp.where(live_mask, jnp.exp(jnp.where(live_mask, score_part - row_max[:, None], 0.0)), 0.0)
        / row_norm[:, None]
    )
    grad_part = loss_scale * KEYS * (softmax_vals - target_prob) / pair_count
    grad_tiles = grad_part.reshape(tiles_here, BLOCK, KEYS)

    def backward(operands):
        query_tile, weight_tile, key_tile, grad_tile = operands
        key_rows = key_tile.reshape(-1, key_width)
        values = dot_values(query_tile, key_tile)
        weight_grad = score_scale * jnp.sum(
            jnp.maximum(values, 0.0) * grad_tile[:, None, :], axis=2
        )
        dot_grads = (
            score_scale
            * weight_tile[:, :, None]
            * grad_tile[:, None, :]
            * (values > 0).astype(jnp.float32)
        ).astype(jnp.bfloat16)
        query_grad = jnp.einsum(
            "qhk,kd->qhd", dot_grads, key_rows, preferred_element_type=jnp.float32
        ).astype(jnp.bfloat16)
        key_grad = jnp.einsum(
            "qhk,qhd->kd", dot_grads, query_tile, preferred_element_type=jnp.float32
        )
        return (query_grad, weight_grad, key_grad.reshape(SLOTS, BLOCK, key_width))

    query_grads, weight_grads, key_parts = lax.map(
        backward, (query_tiles, weight_tiles, fetched, grad_tiles)
    )
    slot_grads = key_parts.reshape(tiles_here * SLOTS, BLOCK, key_width)
    spread = jax.ops.segment_sum(
        slot_grads, table_index.reshape(-1), num_segments=tiles_here + owner_count * CAP
    )
    returned = lax.all_to_all(
        spread[tiles_here:].reshape(owner_count, CAP, BLOCK, key_width).astype(jnp.bfloat16),
        SEQ,
        split_axis=0,
        concat_axis=0,
        tiled=True,
    ).astype(jnp.float32)
    owned_grad = spread[:tiles_here] + jax.ops.segment_sum(
        returned.reshape(owner_count * CAP, BLOCK, key_width),
        asked_slots.reshape(-1),
        num_segments=tiles_here,
    )
    key_grads = over_copies(owned_grad.astype(jnp.bfloat16), "head").astype(jnp.float32)
    return (
        query_grads.reshape(row_count, heads_here, key_width),
        weight_grads.reshape(row_count, heads_here),
        key_grads.reshape(row_count, key_width),
        KEYS * loss_total / pair_count,
    )


def solution(mesh):
    torus = Mesh(
        mesh.devices.reshape(4, 8, 2, mesh.shape["head"]), ("seq_0", "seq_1", "seq_2", "head")
    )
    in_specs = (P(SEQ, "head", None), P(SEQ, "head"), P(SEQ, None), P(SEQ, None), P(SEQ, None), P())
    out_specs = (P(SEQ, "head", None), P(SEQ, "head"), P(SEQ, None), P())
    return jax.shard_map(local, mesh=torus, in_specs=in_specs, out_specs=out_specs, check_vma=False)
```

profile of v0, /device:TPU:1, one launch (start us, length us, event | category | flops | bytes accessed | tf_op | source)
XLA Modules:
  0.0 379.5 jit_solution(12548023386545640363)
XLA Ops:
  11.0 22.1 %all_to_all.27 = s32[64,1,1]{2,1,0:T(1,128)S(1)} all-to-all(s32[64,1,1]{2,1,0:T(1,128)S(1)} %copy.39), channel_id=1, replica_groups=mesh['seq_0'=4,'seq_1'=8,'seq_2'=2,'head'=4] {'seq_0','seq_1','seq_2'}, dimensions={0} | all-to-all | bytes 512 | tf_op jit(solution)/shard_map/all_to_all | solution.py:77
  33.1 2.7 fusion.46
  37.9 5.7 %all-to-all-start.1 = ((bf16[64,1,128,128]{3,2,1,0:T(8,128)(2,1)}), bf16[64,1,128,128]{3,2,1,0:T(8,128)(2,1)}, u32[]{:S(2)}, u32[]{:S(2)}) async-start(bf16[64,1,128,128]{3,2,1,0:T(8,128)(2,1)} %bitcast.22), calls=%async_computation.1 | async-start | bytes 4194304 | tf_op jit(solution)/shard_map/all_to_all | solution.py:79
  45.1 49.8 %all-to-all-done.1 = bf16[64,1,128,128]{3,2,1,0:T(8,128)(2,1)} async-done(((bf16[64,1,128,128]{3,2,1,0:T(8,128)(2,1)}), bf16[64,1,128,128]{3,2,1,0:T(8,128)(2,1)}, u32[]{:S(2)}, u32[]{:S(2)}) %all-to-all-start.1) | async-done | bytes 2097184 | tf_op jit(solution)/shard_map/all_to_all | solution.py:79
  94.9 3.1 pad_maximum_fusion
  100.4 8.3 %while.24 = (s32[]{:T(128)}, f32[2,128,2048]{2,1,0:T(8,128)}, bf16[2,128,16,128]{3,1,2,0:T(8,128)(2,1)S(1)}, bf16[2,16,128,128]{3,2,1,0:T(8,128)(2,1)S(1)}, f32[2,128,16]{1,2,0:T(8,128)S(1)}, /*index=5*/s32[]{:T(128)}) while((s32[]{:T(128)}, f32[2,128,2048]{2,1,0:T(8,128)}, bf16[2,128,16,128]{3,1,2,0:T(8,128)(2,1)S(1)}, ...), condition=%wide.region_6.7_spmd, body=%wide.region_4.6_spmd.sunk | while | flops 1086324736 | bytes 22044820 | solution.py:106
  100.5 2.6 multiply_reduce_fusion.4
  104.6 2.6 multiply_reduce_fusion.4
  112.7 56.5 %all-reduce.6.cloned.1.call-done = f32[256,2048]{1,0:T(8,128)} async-done(((f32[256,2048]{1,0:T(8,128)}), f32[256,2048]{1,0:T(8,128)}) %all-reduce.6.cloned.1.call-update) | async-done | bytes 2097168 | tf_op jit(solution)/shard_map/psum | solution.py:109
  169.2 2.9 select_reduce_fusion.1
  172.1 3.6 select_reduce_fusion
  178.4 8.9 %all-reduce.2 = (f32[]{:T(128)}, f32[]{:T(128)}) all-reduce(f32[]{:T(128)S(6)} %mul.113, f32[]{:T(128)S(6)} %mul.115), channel_id=1, replica_groups=mesh['seq_0'=4,'seq_1'=8,'seq_2'=2,'head'=4] {'seq_0'}, use_global_device_ids=true, to_apply=%region_12.13 | all-reduce | flops 2 | bytes 16 | tf_op jit(solution)/shard_map/psum | solution.py:20
  187.3 14.4 %all-reduce = (f32[]{:T(128)}, f32[]{:T(128)}) all-reduce(f32[]{:T(128)} %get-tuple-element.167, f32[]{:T(128)} %get-tuple-element.168), channel_id=1, replica_groups=mesh['seq_0'=4,'seq_1'=8,'seq_2'=2,'head'=4] {'seq_1'}, use_global_device_ids=true, to_apply=%region_13.14 | all-reduce | flops 2 | bytes 16 | tf_op jit(solution)/shard_map/psum | solution.py:20
  201.7 9.4 %all-reduce.3 = (f32[]{:T(128)}, f32[]{:T(128)}) all-reduce(f32[]{:T(128)} %get-tuple-element.163, f32[]{:T(128)} %get-tuple-element.164), channel_id=1, replica_groups=mesh['seq_0'=4,'seq_1'=8,'seq_2'=2,'head'=4] {'seq_2'}, use_global_device_ids=true, to_apply=%region_14.15 | all-reduce | flops 2 | bytes 16 | tf_op jit(solution)/shard_map/psum | solution.py:20
  211.1 7.4 %all-reduce.1 = (f32[]{:T(128)}, f32[]{:T(128)}) all-reduce(f32[]{:T(128)} %get-tuple-element.169, f32[]{:T(128)} %get-tuple-element.170), channel_id=1, replica_groups=mesh['seq_0'=4,'seq_1'=8,'seq_2'=2,'head'=4] {'head'}, use_global_device_ids=true, to_apply=%region_15.16 | all-reduce | flops 2 | bytes 16 | tf_op jit(solution)/shard_map/psum | solution.py:20
  218.4 4.8 %multiply_divide_fusion = f32[256,2048]{1,0:T(8,128)} fusion(f32[256,2048]{1,0:T(8,128)S(1)} %copy-done.1, bf16[256,2048]{1,0:T(8,128)(2,1)} %param.13, f32[]{:T(128)} %get-tuple-element.165, f32[256]{0:T(256)S(1)} %get-tuple-element.134, f32[256]{0:T(256)S(1)} %get-tuple-element.132, f32[256]{0:T(256)S(1)} %get-tuple-element.133, ...), kind=kLoop, calls=%fused_computation.54 | loop fusion | flops 5767168 | bytes 5770244 | tf_op jit(solution)/shard_map/div | solution.py:129
  223.2 54.7 %while.25 = (s32[]{:T(128)}, bf16[2,128,16,128]{3,2,1,0:T(8,128)(2,1)}, f32[2,128,16]{1,0,2:T(2,128)S(1)}, f32[2,16,128,128]{3,2,1,0:T(8,128)}, bf16[2,128,16,12...) while((s32[]{:T(128)}, ...), condition=%wide.region_18.19_spmd, body=%wide.region_16.18_spmd.sunk | while | flops 3313502208 | bytes 53560508 | solution.py:153
  224.9 7.1 %fusion.74 = (u16[128,2048]{1,0:T(8,128)(2,1)S(1)}, f32[128,16,2048]{2,0,1:T(8,128)}) fusion(bf16[2048,128,1]{1,0,2:T(8,128)(2,1)S(1)} %bitcast.149, bf16[2,128,16,128]{3,1,2,0:T(8,128)(2,1)S(1)} %copy-done.4, s32[]{:T(128)S(6)} %copy.100), kind=kOutput, calls=%fused_computation.21.clone.1 | convolution fusion | flops 1094451200 | bytes 18350084 | tf_op jit(solution)/shard_map/while/body/eval_jaxpr/qhd,kd->qhk/dot_general | solution.py:94
  232.0 3.4 fusion.75
  235.4 7.5 %multiply_reduce_fusion.5 = f32[128,16]{0,1:T(8,128)S(1)} fusion(f32[128,16,2048]{2,0,1:T(8,128)} %get-tuple-element.272, f32[128,2048]{1,0:T(8,128)S(1)} %get-tuple-element.269), kind=kLoop, calls=%fused_computation.19.clone.1 | loop fusion | flops 12580864 | bytes 17833984 | tf_op jit(solution)/shard_map/while/body/eval_jaxpr/reduce_sum | solution.py:136
  245.1 5.4 %fusion.76 = f32[2,16,128,128]{3,2,1,0:T(8,128)} fusion(f32[2,16,128,128]{3,2,1,0:T(8,128)} %get-tuple-element.306, s32[]{:T(128)S(6)} %copy.100, bf16[2,128,16,128]{3,1,2,0:T(8,128)(2,1)} %get-tuple-element.317, f32[2048,128]{0,1:T(8,128)S(1)} %get-tuple-element.273, f32[16,128]{1,0:T(8,128)S(1)} %get-tuple-element.274, u16[128,2048]{1,0:T(8,128)(2,1)} %copy-done.2), kind=kOutput, calls=%fused_computation.28.clone.1 | convolution fusion | flops 1103101952 | bytes 3154944 | tf_op jit(solution)/shard_map/while/body/eval_jaxpr/qhk,qhd->kd/dot_general | solution.py:148
  252.2 7.1 %fusion.74 = (u16[128,2048]{1,0:T(8,128)(2,1)S(1)}, f32[128,16,2048]{2,0,1:T(8,128)}) fusion(bf16[2048,128,1]{1,0,2:T(8,128)(2,1)S(1)} %bitcast.149, bf16[2,128,16,128]{3,1,2,0:T(8,128)(2,1)S(1)} %copy-done.4, s32[]{:T(128)S(6)} %copy.100), kind=kOutput, calls=%fused_computation.21.clone.1 | convolution fusion | flops 1094451200 | bytes 18350084 | tf_op jit(solution)/shard_map/while/body/eval_jaxpr/qhd,kd->qhk/dot_general | solution.py:94
  259.4 3.4 fusion.75
  262.8 7.5 %multiply_reduce_fusion.5 = f32[128,16]{0,1:T(8,128)S(1)} fusion(f32[128,16,2048]{2,0,1:T(8,128)} %get-tuple-element.272, f32[128,2048]{1,0:T(8,128)S(1)} %get-tuple-element.269), kind=kLoop, calls=%fused_computation.19.clone.1 | loop fusion | flops 12580864 | bytes 17833984 | tf_op jit(solution)/shard_map/while/body/eval_jaxpr/reduce_sum | solution.py:136
  272.5 5.4 %fusion.76 = f32[2,16,128,128]{3,2,1,0:T(8,128)} fusion(f32[2,16,128,128]{3,2,1,0:T(8,128)} %get-tuple-element.306, s32[]{:T(128)S(6)} %copy.100, bf16[2,128,16,128]{3,1,2,0:T(8,128)(2,1)} %get-tuple-element.317, f32[2048,128]{0,1:T(8,128)S(1)} %get-tuple-element.273, f32[16,128]{1,0:T(8,128)S(1)} %get-tuple-element.274, u16[128,2048]{1,0:T(8,128)(2,1)} %copy-done.2), kind=kOutput, calls=%fused_computation.28.clone.1 | convolution fusion | flops 1103101952 | bytes 3154944 | tf_op jit(solution)/shard_map/while/body/eval_jaxpr/qhk,qhd->kd/dot_general | solution.py:148
  280.5 7.0 %scatter_fusion = f32[66,128,128]{2,1,0:T(8,128)} fusion(f32[66,128,128]{2,1,0:T(8,128)} %broadcast_in_dim.112, s32[32]{0:T(128)S(1)} %copy-done.13, f32[32,128,128]{2,1,0:T(8,128)S(1)} %bitcast.157), kind=kCustom, calls=%fused_computation.4 | custom fusion | flops 524288 | bytes 6291584 | tf_op jit(solution)/shard_map/scatter-add | solution.py:157
  287.4 3.9 %fusion.37 = bf16[64,1,128,128]{3,2,1,0:T(8,128)(2,1)} fusion(f32[66,128,128]{2,1,0:T(8,128)} %scatter_fusion), kind=kLoop, calls=%fused_computation.50 | loop fusion | bytes 4194304 | tf_op jit(solution)/shard_map/convert_element_type | solution.py:161
  291.3 6.8 %all-to-all-start.2 = ((bf16[64,1,128,128]{3,2,1,0:T(8,128)(2,1)}), bf16[64,1,128,128]{3,2,1,0:T(8,128)(2,1)S(1)}, u32[]{:S(2)}, u32[]{:S(2)}) async-start(bf16[64,1,128,128]{3,2,1,0:T(8,128)(2,1)} %fusion.37), calls=%async_computation.2 | async-start | bytes 4194304 | tf_op jit(solution)/shard_map/all_to_all | solution.py:160
  299.1 50.3 %all-to-all-done.2 = bf16[64,1,128,128]{3,2,1,0:T(8,128)(2,1)S(1)} async-done(((bf16[64,1,128,128]{3,2,1,0:T(8,128)(2,1)}), bf16[64,1,128,128]{3,2,1,0:T(8,128)(2,1)S(1)}, u32[]{:S(2)}, u32[]{:S(2)}) %all-to-all-start.2) | async-done | bytes 2097184 | tf_op jit(solution)/shard_map/all_to_all | solution.py:160
  351.8 8.8 %scatter_fusion.1 = f32[2,128,128]{2,1,0:T(8,128)S(1)} fusion(f32[2,128,128]{2,1,0:T(8,128)S(1)} %slice.17, s32[64]{0:T(128)S(1)} %copy-done.12, f32[64,128,128]{2,1,0:T(8,128)} %bitcast_convert_fusion), kind=kCustom, calls=%fused_computation.5 | custom fusion | flops 1048576 | bytes 12583168 | tf_op jit(solution)/shard_map/scatter-add | solution.py:167
  361.4 3.4 all-to-all-start.3
  366.7 4.1 %all-to-all-done.3 = bf16[4,2,128,128]{3,2,1,0:T(8,128)(2,1)S(1)} async-done(((bf16[4,2,128,128]{3,2,1,0:T(8,128)(2,1)}), bf16[4,2,128,128]{3,2,1,0:T(8,128)(2,1)S(1)}, u32[]{:S(2)}, u32[]{:S(2)}) %all-to-all-start.3) | async-done | bytes 262176 | tf_op jit(solution)/shard_map/all_to_all | solution.py:26
  (103 shorter events, 32.8 us)
Async XLA Ops:
  7.2 28.6 %copy-start = (bf16[256,128]{1,0:T(8,128)(2,1)S(1)}, bf16[256,128]{1,0:T(8,128)(2,1)}, u32[]{:S(2)}) copy-start(bf16[256,128]{1,0:T(8,128)(2,1)} %param.12) | copy-start | bytes 196612
  37.9 6.9 %copy-start.9 = (bf16[256,16,128]{2,1,0:T(8,128)(2,1)S(1)}, bf16[256,16,128]{2,1,0:T(8,128)(2,1)}, u32[]{:S(2)}) copy-start(bf16[256,16,128]{2,1,0:T(8,128)(2,1)} %param.10) | copy-start | bytes 3145732
  37.9 57.0 %all-to-all-start.1 = ((bf16[64,1,128,128]{3,2,1,0:T(8,128)(2,1)}), bf16[64,1,128,128]{3,2,1,0:T(8,128)(2,1)}, u32[]{:S(2)}, u32[]{:S(2)}) async-start(bf16[64,1,128,128]{3,2,1,0:T(8,128)(2,1)} %bitcast.22), calls=%async_computation.1 | async-start | bytes 4194304 | tf_op jit(solution)/shard_map/all_to_all | solution.py:79
  43.7 1.4 copy-start.11
  43.7 125.5 %all-reduce.6.cloned.1.call-start = ((), (), s32[]{:S(2)}) async-start(), calls=%async_computation.4 | async-start | bytes 4194304 | tf_op jit(solution)/shard_map/psum | solution.py:109
  100.5 2.7 copy-start.7
  103.3 1.3 copy-start.8
  104.6 2.7 copy-start.7
  107.4 1.3 copy-start.8
  108.7 3.9 %copy-start.3 = (bf16[2,128,16,128]{3,1,2,0:T(8,128)(2,1)}, bf16[2,128,16,128]{3,1,2,0:T(8,128)(2,1)S(1)}, u32[]{:S(2)}) copy-start(bf16[2,128,16,128]{3,1,2,0:T(8,128)(2,1)S(1)} %get-tuple-element.326) | copy-start | bytes 3145732
  108.7 0.7 copy-start.14
  108.7 0.7 copy-start.10
  169.2 2.9 copy-start.1
  169.2 2.9 copy-start.5
  223.2 1.6 copy-start.4
  232.0 3.4 copy-start.2
  250.6 1.6 copy-start.4
  259.4 3.4 copy-start.2
  277.9 2.5 copy-start.6
  277.9 2.5 copy-start.13
  291.3 58.0 %all-to-all-start.2 = ((bf16[64,1,128,128]{3,2,1,0:T(8,128)(2,1)}), bf16[64,1,128,128]{3,2,1,0:T(8,128)(2,1)S(1)}, u32[]{:S(2)}, u32[]{:S(2)}) async-start(bf16[64,1,128,128]{3,2,1,0:T(8,128)(2,1)} %fusion.37), calls=%async_computation.2 | async-start | bytes 4194304 | tf_op jit(solution)/shard_map/all_to_all | solution.py:160
  299.1 52.7 %copy-start.12 = (s32[64]{0:T(128)S(1)}, s32[64]{0:T(128)}, u32[]{:S(2)}) copy-start(s32[64]{0:T(128)} %get-tuple-element.135) | copy-start | bytes 772
  361.4 9.5 %all-to-all-start.3 = ((bf16[4,2,128,128]{3,2,1,0:T(8,128)(2,1)}), bf16[4,2,128,128]{3,2,1,0:T(8,128)(2,1)S(1)}, u32[]{:S(2)}, u32[]{:S(2)}) async-start(bf16[4,2,128,128]{3,2,1,0:T(8,128)(2,1)} %broadcast_in_dim.113), calls=%async_computation.3 | async-start | bytes 524288 | tf_op jit(solution)/shard_map/all_to_all | solution.py:26
Sparse Core Ops, SparseCore 0:
  108.9 60.2 all-reduce.5
where the time goes:
time: 381 us; the launch traced here: 379 us
  waiting for transfers between devices  161 us (42%)
  blocking collectives  62.1 us (16%)
  other arithmetic  57.1 us (15%)
  matrix products  37.2 us (10%)
  local copies, waits for them, and re-layouts  27.4 us (7%)
  between operations  18.7 us (5%)
  starting transfers between devices  16 us (4%)
    psum x1, waiting for transfers between devices, local(): score_part = lax.psum(partial_value, 'head')  56.5 us
    all_to_all x1, waiting for transfers between devices, local(): lax.all_to_all(spread[tiles_here:].reshape(owner_count, CAP, BLOCK, key_w...  50.3 us
    all_to_all x1, waiting for transfers between devices, local(): lax.all_to_all(reply_blocks, SEQ, split_axis=0, concat_axis=0, tiled=True)  49.8 us
    psum x4, blocking collectives, over_axes(): value = lax.psum(value, axis)  40 us
    all_to_all x1, blocking collectives, local(): lax.all_to_all(request, SEQ, split_axis=0, concat_axis=0, tiled=True)  22.1 us
    dot_general x4, matrix products, dot_values(): jnp.einsum('qhd,kd->qhk', query_tile, key_tile.reshape(-1, key_width), pr...  19.5 us
    reduce_sum x2, other arithmetic, backward(): jnp.sum(jnp.maximum(values, 0.0) * grad_tile[:, None, :], axis=2)  14.9 us
    dot_general x2, matrix products, backward(): jnp.einsum('qhk,qhd->kd', dot_grads, query_tile, preferred_element_type=j...  10.9 us
  transfers between devices with their start and end apart: 4, of which 4 were waited for; matrix products, arithmetic and copies ran while one was open for 1% of the time, Pallas kernels for 0%

commit v1 on v0

v1 whole, which is shorter than its diff:
```python
import functools
import jax
import jax.numpy as jnp
from jax import lax
from jax.experimental import pallas as pl
from jax.experimental.pallas import tpu as pltpu
from jax.sharding import Mesh
from jax.sharding import PartitionSpec as P

BLOCK = 128
SLOTS = 16
KEYS = SLOTS * BLOCK
DH = 128
NY = 4
ROWS = 64
QUARTER = BLOCK // NY
SEQ = ("x", "z", "c")
LOSS_SCALE = 4194304.0
SCORE_SCALE = DH ** (-0.5)
MESH = pl.DeviceIdType.MESH
F32 = jnp.float32
BF16 = jnp.bfloat16


def coords(nx, nz):
    return (lax.axis_index("x"), lax.axis_index("z"), lax.axis_index("c"), lax.axis_index("y"))


def chip_at(nx, nz, x, z, i, sign):
    dx, dz = i // nz, lax.rem(i, nz)
    if sign > 0:
        return lax.rem(x + dx, nx), lax.rem(z + dz, nz)
    return lax.rem(x - dx + nx, nx), lax.rem(z - dz + nz, nz)


def greet(nx, nz, x, z, c, y):
    barrier = pltpu.get_barrier_semaphore()
    for i in range(1, NY):
        pl.semaphore_signal(
            barrier, inc=1, device_id={"y": lax.rem(y + i, NY)}, device_id_type=MESH
        )
    pl.semaphore_signal(barrier, inc=1, device_id={"c": 1 - c}, device_id_type=MESH)

    def one(i, carry):
        px, pz = chip_at(nx, nz, x, z, i, 1)
        pl.semaphore_signal(barrier, inc=1, device_id={"x": px, "z": pz}, device_id_type=MESH)
        return carry

    lax.fori_loop(1, nx * nz, one, 0)
    pl.semaphore_wait(barrier, NY + nx * nz - 1)


def home_of(blocks_s, block):
    base = (block // 4) * 4
    pos = base
    for i in range(1, 4):
        pos = pos + jnp.where(blocks_s[base + i] == block, i, 0)
    return pos


def gather_kernel(
    nx, nz, q_ref, w_ref, pay_ref, chosen_s, blocks_s,
    qx, wx, kx, cnt,
    gath, sel, lsem, qs, qr, ws, wr, ps, pr, cs, cr, ks, kr,
):
    chips = nx * nz
    x, z, c, y = coords(nx, nz)
    me = x * nz + z
    greet(nx, nz, x, z, c, y)

    def y_peer(i):
        return {"y": lax.rem(y + i, NY)}

    def q_copy(i):
        return pltpu.make_async_remote_copy(
            src_ref=q_ref.at[lax.rem(y + i, NY)], dst_ref=qx.at[y],
            send_sem=qs.at[i - 1], recv_sem=qr.at[i - 1],
            device_id=y_peer(i), device_id_type=MESH,
        )

    def w_copy(i):
        return pltpu.make_async_remote_copy(
            src_ref=w_ref.at[lax.rem(y + i, NY)], dst_ref=wx.at[y],
            send_sem=ws.at[i - 1], recv_sem=wr.at[i - 1],
            device_id=y_peer(i), device_id_type=MESH,
        )

    def plane_copy(i):
        px, pz = chip_at(nx, nz, x, z, i, 1)
        return pltpu.make_async_remote_copy(
            src_ref=pay_ref, dst_ref=gath.at[c * chips + me],
            send_sem=ps.at[i], recv_sem=pr.at[i],
            device_id={"x": px, "z": pz}, device_id_type=MESH,
        )

    def core_copy(i):
        sx, sz = chip_at(nx, nz, x, z, i, -1)
        slot = c * chips + sx * nz + sz
        return pltpu.make_async_remote_copy(
            src_ref=gath.at[slot], dst_ref=gath.at[slot],
            send_sem=cs.at[i], recv_sem=cr.at[i],
            device_id={"c": 1 - c}, device_id_type=MESH,
        )

    def own_copy():
        return pltpu.make_async_remote_copy(
            src_ref=pay_ref, dst_ref=gath.at[c * chips + me],
            send_sem=cs.at[0], recv_sem=cr.at[0],
            device_id={"c": 1 - c}, device_id_type=MESH,
        )

    lax.fori_loop(1, chips, lambda i, k: (plane_copy(i).start(), k)[1], 0)
    own_copy().start()
    for i in range(1, NY):
        w_copy(i).start()
    for i in range(1, NY):
        q_copy(i).start()
    own_q = pltpu.make_async_copy(q_ref.at[y], qx.at[y], lsem)
    own_q.start()
    wx[y] = w_ref[y]
    gath[c * chips + me] = pay_ref[...]

    def relay(i, carry):
        plane_copy(i).wait_recv()
        core_copy(i).start()
        return carry

    lax.fori_loop(1, chips, relay, 0)
    lax.fori_loop(0, chips, lambda i, k: (core_copy(i).wait_recv(), k)[1], 0)

    for tile in range(2):
        for j in range(SLOTS):
            pos = home_of(blocks_s, jnp.maximum(chosen_s[tile, j], 0))
            device = pos // 2
            slot = lax.rem(device, 2) * chips + device // 2
            part = 2 * lax.rem(pos, 2)
            sel[tile, j, 0:16] = gath[slot, part]
            sel[tile, j, 16:32] = gath[slot, part + 1]

    def k_copy(i):
        peer = lax.rem(y + i, NY)
        return pltpu.make_async_remote_copy(
            src_ref=sel.at[peer // 2], dst_ref=kx.at[:, pl.ds(pl.multiple_of(y * QUARTER, QUARTER), QUARTER), :],
            send_sem=ks.at[i - 1], recv_sem=kr.at[i - 1],
            device_id={"y": peer}, device_id_type=MESH,
        )

    for i in range(1, NY):
        k_copy(i).start()
    kx[:, pl.ds(pl.multiple_of(y * QUARTER, QUARTER), QUARTER), :] = sel[y // 2]

    def add_count(i, total):
        return total + gath[i, 4].astype(F32)

    total = lax.fori_loop(0, 2 * chips, add_count, jnp.zeros((16, 128), F32))
    tiles = 4 * chips
    cnt[...] = total[0:8] * float(BLOCK * BLOCK) - float(
        tiles * (BLOCK * BLOCK - BLOCK * (BLOCK + 1) // 2)
    )

    own_q.wait()
    own_copy().wait_send()
    lax.fori_loop(1, chips, lambda i, k: (plane_copy(i).wait_send(), core_copy(i).wait_send(), k)[2], 0)
    for i in range(1, NY):
        w_copy(i).wait()
        q_copy(i).wait()
        k_copy(i).wait()


def split3(value):
    hi = value.astype(BF16)
    rest = value - hi.astype(F32)
    mid = rest.astype(BF16)
    lo = (rest - mid.astype(F32)).astype(BF16)
    return hi.astype(F32), mid.astype(F32), lo.astype(F32)


def loss_rows(value, rows):
    hi, mid, lo = split3(value)
    row = lax.broadcasted_iota(jnp.int32, (rows, 128), 0)
    out = jnp.where(row == 0, hi, jnp.where(row == 1, mid, jnp.where(row == 2, lo, 0.0)))
    return out.astype(BF16)


def compute_kernel(
    nx, nz, q_ref, wb_ref, k_ref, t_ref, cnt_ref, chosen_s, blocks_s,
    qg, wg, dks, inv,
    kt, qt, dots, sc, gs, dkt, tgt, tsem,
):
    positions = 4 * nx * nz
    y = lax.axis_index("y")
    tile = y // 2
    tcopy = pltpu.make_async_copy(t_ref.at[y], tgt, tsem)
    tcopy.start()
    for j in range(SLOTS):
        kt[:, j * BLOCK : (j + 1) * BLOCK] = k_ref[j * BLOCK : (j + 1) * BLOCK, :].T
    for g in range(NY):
        for b in range(8):
            rows = slice(b * 128, (b + 1) * 128)
            wq = (q_ref[g, rows, :].astype(F32) * wb_ref[g, rows, :]).astype(BF16)
            qt[g, :, rows] = wq.T

    def forward(cc, carry):
        cols = pl.ds(pl.multiple_of(cc * 256, 256), 256)
        keys_t = kt[:, cols]
        for tb in range(4):
            rows = slice(tb * 256, (tb + 1) * 256)
            acc = None
            for g in range(NY):
                d = jnp.dot(q_ref[g, rows, :], keys_t, preferred_element_type=F32)
                dots[g, rows, cols] = d.astype(BF16)
                wv = wb_ref[g, rows, :]
                term = jnp.maximum(d, 0.0) * jnp.concatenate([wv, wv], axis=1)
                acc = term if acc is None else acc + term
            sc[tb * 16 : (tb + 1) * 16, cols] = (
                jnp.sum(acc.reshape(16, 16, 256), axis=1) * SCORE_SCALE
            )
        return carry

    lax.fori_loop(0, KEYS // 256, forward, 0)

    def clear(i, carry):
        inv[0, i] = 2 * SLOTS
        inv[1, i] = 2 * SLOTS
        return carry

    lax.fori_loop(0, positions, clear, 0)

    def enter(i, carry):
        ti, j = i // SLOTS, lax.rem(i, SLOTS)
        block = chosen_s[ti, j]

        @pl.when(block >= 0)
        def _():
            inv[ti, home_of(blocks_s, block)] = i

        return carry

    lax.fori_loop(0, 2 * SLOTS, enter, 0)

    tcopy.wait()
    row = lax.broadcasted_iota(jnp.int32, (ROWS, BLOCK), 0) + ROWS * lax.rem(y, 2)
    col = lax.broadcasted_iota(jnp.int32, (ROWS, BLOCK), 1)

    def live(j):
        on = jnp.where(chosen_s[tile, j] >= 0, 1, 0)
        on = jnp.full((ROWS, BLOCK), on, jnp.int32)
        if j == 0:
            on = jnp.where(col <= row, on, 0)
        return on > 0

    def part(j):
        return slice(j * BLOCK, (j + 1) * BLOCK)

    top = None
    tsum = None
    for j in range(SLOTS):
        s = jnp.where(live(j), sc[:, part(j)], -1e30)
        t = jnp.where(live(j), tgt[:, part(j)].astype(F32), 0.0)
        top = s if top is None else jnp.maximum(top, s)
        tsum = t if tsum is None else tsum + t
    row_max = jnp.max(top, axis=1, keepdims=True)
    row_t = 1.0 / jnp.sum(tsum, axis=1, keepdims=True)
    esum = None
    for j in range(SLOTS):
        e = jnp.where(live(j), jnp.exp(jnp.where(live(j), sc[:, part(j)] - row_max, 0.0)), 0.0)
        gs[:, part(j)] = e
        esum = e if esum is None else esum + e
    norm = jnp.sum(esum, axis=1, keepdims=True)
    row_n = 1.0 / norm
    lse = row_max + jnp.log(norm)
    kl = None
    for j in range(SLOTS):
        on = live(j)
        prob = jnp.where(on, tgt[:, part(j)].astype(F32) * row_t, 0.0)
        term = jnp.where(
            on, prob * (jnp.log(jnp.where(on, prob, 1.0)) - sc[:, part(j)] + lse), 0.0
        )
        kl = term if kl is None else kl + term
        gs[:, part(j)] = gs[:, part(j)] * row_n - prob
    kl_row = jnp.sum(kl, axis=0, keepdims=True)
    kl_sum = jnp.broadcast_to(jnp.sum(kl_row, axis=1, keepdims=True), (1, 128))

    scale = (LOSS_SCALE * KEYS * SCORE_SCALE) / cnt_ref[0:1, :]

    for g in range(NY):
        for t in range(ROWS):
            rows = slice(t * 16, (t + 1) * 16)
            grad = jnp.broadcast_to(gs[t : t + 1, :], (16, KEYS)).astype(BF16)
            d = dots[g, rows, :]
            dots[g, rows, :] = jnp.where(d > 0, grad, jnp.zeros_like(grad))
        a = jnp.dot(dots[g], k_ref[...], preferred_element_type=F32) * scale
        qg[g] = (a * wb_ref[g]).astype(BF16)
        wg[g] = jnp.sum((a * q_ref[g].astype(F32)).reshape(ROWS, 16, DH), axis=2)
        part_t = jnp.dot(qt[g], dots[g], preferred_element_type=F32)
        if g == 0:
            dkt[...] = part_t
        else:
            dkt[...] += part_t

    for j in range(SLOTS):
        block = (dkt[:, part(j)].T * scale).astype(BF16)
        for i in range(NY):
            dks[i, j] = block[i * QUARTER : (i + 1) * QUARTER]
    lr = loss_rows(kl_sum, QUARTER)
    for i in range(NY):
        dks[i, SLOTS] = lr


def scatter_kernel(
    nx, nz, qg_ref, wg_ref, dks_ref, inv_s, cnt_ref,
    oq, ow, ok, ol,
    yrecv, table, dsend, drecv, lsend, lrecv, pay, precv, fin,
    lsem, qs, qr, ws, wr, ds_, dr, cs, cr, ls, lr, ps, pr, fs, fr,
):
    chips = nx * nz
    x, z, c, y = coords(nx, nz)
    me = x * nz + z
    greet(nx, nz, x, z, c, y)

    def y_copy(src, dst, send, recv, i):
        return pltpu.make_async_remote_copy(
            src_ref=src.at[lax.rem(y + i, NY)], dst_ref=dst.at[y],
            send_sem=send.at[i - 1], recv_sem=recv.at[i - 1],
            device_id={"y": lax.rem(y + i, NY)}, device_id_type=MESH,
        )

    def d_copy(i):
        return y_copy(dks_ref, yrecv, ds_, dr, i)

    def q_copy(i):
        return y_copy(qg_ref, oq, qs, qr, i)

    def w_copy(i):
        return y_copy(wg_ref, ow, ws, wr, i)

    for i in range(1, NY):
        d_copy(i).start()
    for i in range(1, NY):
        w_copy(i).start()
    for i in range(1, NY):
        q_copy(i).start()
    own_q = pltpu.make_async_copy(qg_ref.at[y], oq.at[y], lsem)
    own_q.start()
    ow[y] = wg_ref[y]
    yrecv[y] = dks_ref[y]
    table[2 * SLOTS] = jnp.zeros((QUARTER, DH), F32)
    for i in range(1, NY):
        d_copy(i).wait_recv()
    for tile in range(2):
        for j in range(SLOTS):
            table[tile * SLOTS + j] = yrecv[2 * tile, j].astype(F32) + yrecv[
                2 * tile + 1, j
            ].astype(F32)
    loss4 = yrecv[0, SLOTS].astype(F32)
    for i in range(1, NY):
        loss4 = loss4 + yrecv[i, SLOTS].astype(F32)
    loss_here = jnp.sum(loss4, axis=0, keepdims=True)

    def dense(core, chip, l):
        pos = (chip * 2 + core) * 2 + l
        return table[inv_s[0, pos]] + table[inv_s[1, pos]]

    def fill(chip, carry):
        for l in range(2):
            v = dense(1 - c, chip, l).astype(BF16)
            dsend[chip, l] = v
        return carry

    lax.fori_loop(0, chips, fill, 0)
    lsend[...] = jnp.broadcast_to(loss_here, (8, 128))

    def core_copy():
        return pltpu.make_async_remote_copy(
            src_ref=dsend, dst_ref=drecv, send_sem=cs, recv_sem=cr,
            device_id={"c": 1 - c}, device_id_type=MESH,
        )

    def loss_copy():
        return pltpu.make_async_remote_copy(
            src_ref=lsend, dst_ref=lrecv, send_sem=ls, recv_sem=lr,
            device_id={"c": 1 - c}, device_id_type=MESH,
        )

    loss_copy().start()
    core_copy().start()
    loss_copy().wait_recv()
    lrows = loss_rows(loss_here + lrecv[0:1, :], 16)
    core_copy().wait_recv()

    def merge(chip, carry):
        for l in range(2):
            v = dense(c, chip, l) + drecv[chip, l].astype(F32)
            v = v.astype(BF16)
            pay[chip, 2 * l] = v[0:16]
            pay[chip, 2 * l + 1] = v[16:32]
        pay[chip, 4] = lrows
        return carry

    lax.fori_loop(0, chips, merge, 0)

    def plane_copy(i):
        px, pz = chip_at(nx, nz, x, z, i, 1)
        return pltpu.make_async_remote_copy(
            src_ref=pay.at[px * nz + pz], dst_ref=precv.at[me],
            send_sem=ps.at[i], recv_sem=pr.at[i],
            device_id={"x": px, "z": pz}, device_id_type=MESH,
        )

    lax.fori_loop(1, chips, lambda i, k: (plane_copy(i).start(), k)[1], 0)
    precv[me] = pay[me]
    lax.fori_loop(1, chips, lambda i, k: (plane_copy(i).wait_recv(), k)[1], 0)

    def add(i, total):
        return tuple(total[k] + precv[i, k].astype(F32) for k in range(5))

    total = lax.fori_loop(0, chips, add, tuple(jnp.zeros((16, DH), F32) for _ in range(5)))
    loss_all = jnp.sum(total[4], axis=0, keepdims=True)
    ol[...] = jnp.broadcast_to(loss_all, (8, 128)) * float(KEYS) / cnt_ref[...]
    for l in range(2):
        fin[l, 0:16] = total[2 * l]
        fin[l, 16:32] = total[2 * l + 1]
    mine = pl.ds(pl.multiple_of(y * QUARTER, QUARTER), QUARTER)

    def f_copy(i):
        return pltpu.make_async_remote_copy(
            src_ref=fin, dst_ref=ok.at[:, mine, :],
            send_sem=fs.at[i - 1], recv_sem=fr.at[i - 1],
            device_id={"y": lax.rem(y + i, NY)}, device_id_type=MESH,
        )

    for i in range(1, NY):
        f_copy(i).start()
    ok[:, mine, :] = fin[...]
    own_q.wait()
    core_copy().wait_send()
    loss_copy().wait_send()
    lax.fori_loop(1, chips, lambda i, k: (plane_copy(i).wait_send(), k)[1], 0)
    for i in range(1, NY):
        d_copy(i).wait_send()
        w_copy(i).wait()
        q_copy(i).wait()
        f_copy(i).wait()


VM = pl.BlockSpec(memory_space=pltpu.VMEM)
SM = pl.BlockSpec(memory_space=pltpu.SMEM)
ANY = pl.BlockSpec(memory_space=pl.ANY)
DMA = pltpu.SemaphoreType.DMA


def shape(*dims_dtype):
    return jax.ShapeDtypeStruct(dims_dtype[:-1], dims_dtype[-1])


def local(nx, nz, queries, head_weights, keys, targets, chosen, tile_block):
    chips = nx * nz
    y = lax.axis_index("y")
    heads = queries.shape[1]
    q4 = queries.reshape(NY, ROWS, heads, DH)
    w4 = head_weights.reshape(NY, ROWS, heads)
    quarter = lax.dynamic_slice_in_dim(keys.reshape(2, BLOCK, DH), y * QUARTER, QUARTER, 1)
    live_here = jnp.sum((chosen >= 0).astype(F32)).astype(BF16)
    payload = jnp.concatenate(
        [quarter.reshape(4, 16, DH), jnp.broadcast_to(live_here, (1, 16, DH))], axis=0
    )
    qx, wx, kx, cnt = pl.pallas_call(
        functools.partial(gather_kernel, nx, nz),
        out_shape=[
            shape(NY, ROWS, heads, DH, BF16),
            shape(NY, ROWS, heads, BF16),
            shape(SLOTS, BLOCK, DH, BF16),
            shape(8, 128, F32),
        ],
        in_specs=[ANY, VM, VM, SM, SM],
        out_specs=[VM, VM, VM, VM],
        scratch_shapes=[
            pltpu.VMEM((2 * chips, 5, 16, DH), BF16),
            pltpu.VMEM((2, SLOTS, QUARTER, DH), BF16),
            DMA, DMA((3,)), DMA((3,)), DMA((3,)), DMA((3,)),
            DMA((chips,)), DMA((chips,)), DMA((chips,)), DMA((chips,)),
            DMA((3,)), DMA((3,)),
        ],
        compiler_params=pltpu.CompilerParams(collective_id=0, has_side_effects=True),
        name="gather",
    )(q4, w4, payload, chosen, tile_block)
    wb = jnp.broadcast_to(wx.astype(F32)[..., None], (NY, ROWS, heads, DH))
    wb = wb.reshape(NY, ROWS * heads, DH)
    qf = qx.reshape(NY, ROWS * heads, DH)
    qg, wg, dks, inv = pl.pallas_call(
        functools.partial(compute_kernel, nx, nz),
        out_shape=[
            shape(NY, ROWS * heads, DH, BF16),
            shape(NY, ROWS, heads, F32),
            shape(NY, SLOTS + 1, QUARTER, DH, BF16),
            shape(2, 4 * chips, jnp.int32),
        ],
        in_specs=[VM, VM, VM, ANY, VM, SM, SM],
        out_specs=[VM, VM, VM, SM],
        scratch_shapes=[
            pltpu.VMEM((DH, KEYS), BF16),
            pltpu.VMEM((NY, DH, ROWS * heads), BF16),
            pltpu.VMEM((NY, ROWS * heads, KEYS), BF16),
            pltpu.VMEM((ROWS, KEYS), F32),
            pltpu.VMEM((ROWS, KEYS), F32),
            pltpu.VMEM((DH, KEYS), F32),
            pltpu.VMEM((ROWS, KEYS), BF16),
            DMA,
        ],
        compiler_params=pltpu.CompilerParams(vmem_limit_bytes=60 * 1024 * 1024),
        name="compute",
    )(qf, wb, kx.reshape(KEYS, DH), targets.reshape(NY, ROWS, KEYS), cnt, chosen, tile_block)
    oq, ow, ok, ol = pl.pallas_call(
        functools.partial(scatter_kernel, nx, nz),
        out_shape=[
            shape(NY, ROWS, heads, DH, BF16),
            shape(NY, ROWS, heads, F32),
            shape(2, BLOCK, DH, F32),
            shape(8, 128, F32),
        ],
        in_specs=[ANY, VM, VM, SM, VM],
        out_specs=[VM, VM, VM, VM],
        scratch_shapes=[
            pltpu.VMEM((NY, SLOTS + 1, QUARTER, DH), BF16),
            pltpu.VMEM((2 * SLOTS + 1, QUARTER, DH), F32),
            pltpu.VMEM((chips, 2, QUARTER, DH), BF16),
            pltpu.VMEM((chips, 2, QUARTER, DH), BF16),
            pltpu.VMEM((8, 128), F32),
            pltpu.VMEM((8, 128), F32),
            pltpu.VMEM((chips, 5, 16, DH), BF16),
            pltpu.VMEM((chips, 5, 16, DH), BF16),
            pltpu.VMEM((2, QUARTER, DH), F32),
            DMA, DMA((3,)), DMA((3,)), DMA((3,)), DMA((3,)), DMA((3,)), DMA((3,)),
            DMA, DMA, DMA, DMA, DMA((chips,)), DMA((chips,)), DMA((3,)), DMA((3,)),
        ],
        compiler_params=pltpu.CompilerParams(collective_id=1, has_side_effects=True),
        name="scatter",
    )(qg.reshape(NY, ROWS, heads, DH), wg, dks, inv, cnt)
    rows = NY * ROWS
    return (
        oq.reshape(rows, heads, DH),
        ow.reshape(rows, heads),
        ok.reshape(rows, DH),
        ol[0, 0],
    )


def solution(mesh):
    nx, nz = 4, mesh.shape["seq"] // 8
    torus = Mesh(mesh.devices.reshape(nx, nz, 2, mesh.shape["head"]), ("x", "z", "c", "y"))
    in_specs = (P(SEQ, "y", None), P(SEQ, "y"), P(SEQ, None), P(SEQ, None), P(SEQ, None), P())
    out_specs = (P(SEQ, "y", None), P(SEQ, "y"), P(SEQ, None), P())
    return jax.shard_map(
        functools.partial(local, nx, nz),
        mesh=torus, in_specs=in_specs, out_specs=out_specs, check_vma=False,
    )
```

time: 381 us -> 117 us (0.31)
  waiting for transfers between devices: 161 us -> 0 us
  Pallas kernels: 0 us -> 103 us
  blocking collectives: 62.1 us -> 0 us
  other arithmetic: 57.1 us -> 1.32 us
  matrix products: 37.2 us -> 0 us
  between operations: 18.7 us -> 0.68 us
  starting transfers between devices: 16 us -> 0 us
  local copies, waits for them, and re-layouts: 27.4 us -> 11.4 us
    all_to_all x3 -> x0, waiting for transfers between devices: 104 us -> none  [the longest x1 50.3 us: local(): lax.all_to_all(spread[tiles_here:].reshape(owner_count, CAP, BLOCK, key_w...]
    pallas_call x0 -> x3, Pallas kernels: none -> 103 us  [the longest x1 41.4 us: local(): pl.pallas_call(functools.partial(gather_kernel, nx, nz), out_shape=[shape...]
    psum x1 -> x0, waiting for transfers between devices: 56.5 us -> none  [local(): score_part = lax.psum(partial_value, 'head')]
    psum x4 -> x0, blocking collectives: 40 us -> none  [over_axes(): value = lax.psum(value, axis)]
    dot_general x8 -> x0, matrix products: 37.2 us -> none  [the longest x4 19.5 us: dot_values(): jnp.einsum('qhd,kd->qhk', query_tile, key_tile.reshape(-1, key_width), pr...]
    all_to_all x1 -> x0, blocking collectives: 22.1 us -> none  [local(): lax.all_to_all(request, SEQ, split_axis=0, concat_axis=0, tiled=True)]
    reduce_sum x7 -> x1, other arithmetic: 22 us -> 1.32 us  [local(): live_here = jnp.sum((chosen >= 0).astype(F32)).astype(BF16)]
    all_to_all x3 -> x0, starting transfers between devices: 16 us -> none  [the longest x1 6.84 us: local(): lax.all_to_all(spread[tiles_here:].reshape(owner_count, CAP, BLOCK, key_w...]
  transfers between devices with their start and end apart: 4 -> 0, of which waited for: 4 -> 0; matrix products, arithmetic and copies ran while one was open for 1% -> 0% of each run, Pallas kernels for 0% -> 0%
where the time goes in v1:
time: 117 us; the launch traced here: 116 us
  Pallas kernels  103 us (88%)
  local copies, waits for them, and re-layouts  11.4 us (10%)
  other arithmetic  1.32 us (1%)
    pallas_call x1, Pallas kernels, local(): pl.pallas_call(functools.partial(gather_kernel, nx, nz), out_shape=[shape...  41.4 us
    pallas_call x1, Pallas kernels, local(): pl.pallas_call(functools.partial(scatter_kernel, nx, nz), out_shape=[shap...  40.8 us
    pallas_call x1, Pallas kernels, local(): pl.pallas_call(functools.partial(compute_kernel, nx, nz), out_shape=[shap...  20.7 us
    unnamed x8, local copies, waits for them, and re-layouts  6.05 us
    broadcast_in_dim x2, local copies, waits for them, and re-layouts, local(): wb = jnp.broadcast_to(wx.astype(F32)[..., None], (NY, ROWS, heads, DH))  2.91 us

profile of v1, /device:TPU:1, one launch (start us, length us, event | category | flops | bytes accessed | tf_op | source)
XLA Modules:
  0.0 116.3 jit_solution(14450822935091628044)
XLA Ops:
  0.6 0.0 copy-start
  0.6 1.3 %fusion = bf16[]{:T(256)} fusion(s32[2,16]{1,0:T(2,128)} %chosen_s.3), kind=kLoop, calls=%fused_computation.1 | loop fusion | flops 95 | bytes 130 | tf_op jit(solution)/shard_map/reduce_sum | solution.py:463
  2.0 0.0 copy-done
  2.0 1.3 %concatenate.3.pay_ref = bf16[5,16,128]{2,1,0:T(8,128)(2,1)} pad(bf16[4,16,128]{2,1,0:T(8,128)(2,1)S(1)} %bitcast.22, bf16[]{:T(256)} %fusion), padding=0_1x0_0x0_0 | pad | bytes 36866 | tf_op jit(solution)/shard_map/concatenate | solution.py:464
  3.2 1.4 %copy.12 = bf16[256,16]{1,0:T(8,128)(2,1)} copy(bf16[256,16]{0,1:T(8,128)(2,1)} %param.7) | data formatting | bytes 16384 | tf_op args[1]
  4.7 41.4 %gather.1 = (bf16[4,64,16,128]{3,2,1,0:T(8,128)(2,1)}, bf16[4,64,16]{2,1,0:T(8,128)(2,1)}, bf16[16,128,128]{2,1,0:T(8,128)(2,1)}, f32[8,128]{1,0:T(8,128)}) custom-call(bf16[4,64,16,128]{3,2,1,0:T(8,128)(2,1)} %bitcast.13, bf16[4,64,16]{2,1,0:T(8,128)(2,1)} %bitcast.19, bf16[5,16,128]{2,1,0:T(8,128)(2,1)} %concatenate.3.pay_ref, s32[2,16]{1,0:T(2,128)} %chosen_s.3, ...), custom_call_target="tpu_custom_call" | custom-call | tf_op jit(solution)/shard_map/gather/pallas_call | solution.py:467
  46.1 1.0 reshape.57
  47.0 1.9 %broadcast_in_dim.13.wb_ref = f32[4,1024,128]{2,1,0:T(8,128)} broadcast(f32[4,1024]{1,0:T(4,128)S(1)} %reshape.57), dimensions={0,1} | broadcast | bytes 2113536 | tf_op jit(solution)/shard_map/broadcast_in_dim | solution.py:487
  49.0 20.7 %compute.1 = (bf16[4,1024,128]{2,1,0:T(8,128)(2,1)}, f32[4,64,16]{2,1,0:T(8,128)}, bf16[4,17,32,128]{3,2,1,0:T(8,128)(2,1)}, s32[2,128]{1,0:T(2,128)}) custom-call(bf16[4,1024,128]{2,1,0:T(8,128)(2,1)} %bitcast.17, f32[4,1024,128]{2,1,0:T(8,128)} %broadcast_in_dim.13.wb_ref, bf16[2048,128]{1,0:T(8,128)(2,1)} %bitcast.18, bf16[4,64,2048]{2,1,0:T(8,128)(2,1)} %bitcast.16, ...), custom_call_target="tpu_custom_call" | custom-call | tf_op jit(solution)/shard_map/compute/pallas_call | solution.py:490
  69.7 40.8 %scatter.1 = (bf16[4,64,16,128]{3,2,1,0:T(8,128)(2,1)}, f32[4,64,16]{2,1,0:T(8,128)}, f32[2,128,128]{2,1,0:T(8,128)}, f32[8,128]{1,0:T(8,128)}) custom-call(bf16[4,64,16,128]{3,2,1,0:T(8,128)(2,1)} %bitcast.14, f32[4,64,16]{2,1,0:T(8,128)} %get-tuple-element.21.wg_ref, bf16[4,17,32,128]{3,2,1,0:T(8,128)(2,1)} %get-tuple-element.22.dks_ref, ...), custom_call_target="tpu_custom_call" | custom-call | tf_op jit(solution)/shard_map/scatter/pallas_call | solution.py:513
  110.5 0.0 copy-start.1
  110.5 1.2 %slice.3 = f32[1,1]{1,0:T(1,128)} slice(f32[8,128]{1,0:T(8,128)} %get-tuple-element.27), slice={[0:1], [0:1]} | slice | bytes 8 | tf_op jit(solution)/shard_map/slice | solution.py:544
  111.7 1.6 %copy.13 = f32[256,16]{0,1:T(8,128)} copy(f32[256,16]{1,0:T(8,128)} %bitcast.20) | data formatting | bytes 32768
  113.3 2.4 %copy.16 = bf16[256,16,128]{2,1,0:T(8,128)(2,1)} copy(bf16[256,16,128]{2,1,0:T(8,128)(2,1)} %bitcast.15) | data formatting | bytes 2097152
  115.7 0.0 copy-done.1
  115.7 0.7 copy.17
  (1 shorter events, 0.0 us)
Async XLA Ops:
  0.6 1.3 %copy-start = (bf16[256,128]{1,0:T(8,128)(2,1)S(1)}, bf16[256,128]{1,0:T(8,128)(2,1)}, u32[]{:S(2)}) copy-start(bf16[256,128]{1,0:T(8,128)(2,1)} %param.8) | copy-start | bytes 196612
  110.5 5.2 %copy-start.1 = (f32[2,128,128]{2,1,0:T(8,128)S(1)}, f32[2,128,128]{2,1,0:T(8,128)}, u32[]{:S(2)}) copy-start(f32[2,128,128]{2,1,0:T(8,128)} %get-tuple-element.26) | copy-start | bytes 393220

commit v2 on v0

v2 whole, which is shorter than its diff:
```python
import functools
import jax
import jax.numpy as jnp
from jax import lax
from jax.experimental import pallas as pl
from jax.experimental.pallas import tpu as pltpu
from jax.sharding import Mesh
from jax.sharding import PartitionSpec as P

BLOCK = 128
SLOTS = 16
KEYS = SLOTS * BLOCK
DH = 128
NY = 4
ROWS = 64
HG = 16
RG = ROWS * HG
QUARTER = BLOCK // NY
SEQ = ("x", "z", "c")
LOSS_SCALE = 4194304.0
SCORE_SCALE = DH ** (-0.5)
MESH = pl.DeviceIdType.MESH
F32 = jnp.float32
BF16 = jnp.bfloat16
DMA = pltpu.SemaphoreType.DMA


def remote(src, dst, send, recv, device):
    return pltpu.make_async_remote_copy(
        src_ref=src, dst_ref=dst, send_sem=send, recv_sem=recv,
        device_id=device, device_id_type=MESH,
    )


def loop(lo, hi, body):
    def step(i, carry):
        body(i)
        return carry

    lax.fori_loop(lo, hi, step, 0)


class RowSum:
    def __init__(self, axis, size, refs):
        self.axis, self.size = axis, size
        self.row, self.got, self.send, self.recv = refs

    def copy(self, i):
        peer = lax.rem(lax.axis_index(self.axis) + i, self.size)
        return remote(
            self.row, self.got.at[i], self.send.at[i], self.recv.at[i], {self.axis: peer}
        )

    def start(self, value):
        self.row[...] = value
        for i in range(1, self.size):
            self.copy(i).start()

    def finish(self):
        total = self.row[...]
        for i in range(1, self.size):
            self.copy(i).wait_recv()
            total = total + self.got[i]
        return total

    def drain(self):
        for i in range(1, self.size):
            self.copy(i).wait_send()


def row_sum_scratch(size):
    return [
        pltpu.VMEM((1, 128), F32), pltpu.VMEM((size, 1, 128), F32), DMA((size,)), DMA((size,)),
    ]


def kernel(
    nx, nz, q_ref, w_ref, keys_ref, t_ref, chosen_s, blocks_s,
    oq, ow, ok, ol,
    gath, sel, qx, wx, kx, wb, qt, kt, dots, sc, gs, tgt, qg, wg, wgr, inv,
    dks, yrecv, table, dsend, drecv, pay, xrecv, zsend, zrecv, fin,
    tsem, lsem, osem, qs, qr, ws, wr, zs, zr, xs, xr, cs, cr, ks, kr,
    ds_, dr, gs_, gr, vs, vr, es, er, us, ur, hs, hr, fs, fr, *sums,
):
    chips = nx * nz
    x, z, c, y = (lax.axis_index(a) for a in ("x", "z", "c", "y"))
    other = {"c": 1 - c}
    mine = pl.ds(pl.multiple_of(y * QUARTER, QUARTER), QUARTER)
    sizes = [("z", nz), ("x", nx), ("c", 2), ("y", NY), ("z", nz), ("x", nx), ("c", 2)]
    rows_of = [
        RowSum(a, n, sums[4 * i : 4 * i + 4]) for i, (a, n) in enumerate(sizes)
    ]
    count_z, count_x, count_c, loss_y, loss_z, loss_x, loss_c = rows_of

    def near(k):
        odd = lax.rem(k, 2)
        return odd * ((k + 1) // 2) + (1 - odd) * lax.rem(nz - k // 2, nz)

    def wrap(v, n):
        return lax.rem(v + n, n)

    barrier = pltpu.get_barrier_semaphore()
    for axis, size in (("z", nz), ("x", nx), ("y", NY), ("c", 2)):
        for i in range(1, size):
            peer = lax.rem(lax.axis_index(axis) + i, size)
            pl.semaphore_signal(barrier, inc=1, device_id={axis: peer}, device_id_type=MESH)
    tcopy = pltpu.make_async_copy(t_ref.at[y], tgt, tsem)
    tcopy.start()
    own_q = pltpu.make_async_copy(q_ref.at[y], qx.at[y], lsem)
    own_q.start()
    live_here = 0
    for tile in range(2):
        for j in range(SLOTS):
            live_here = live_here + jnp.where(chosen_s[tile, j] >= 0, 1, 0)
    pl.semaphore_wait(barrier, nz + nx + NY + 2 - 4)

    def slot(core, cx, cz):
        return core * chips + cx * nz + cz

    here = slot(c, x, z)

    def z_copy(dz):
        return remote(
            keys_ref.at[:, mine, :], gath.at[here], zs.at[dz], zr.at[dz],
            {"z": lax.rem(z + dz, nz)},
        )

    def x_copy(dx, dz):
        at = slot(c, x, wrap(z - dz, nz))
        i = dx * nz + dz
        return remote(gath.at[at], gath.at[at], xs.at[i], xr.at[i], {"x": lax.rem(x + dx, nx)})

    def x_own(dx):
        return remote(
            keys_ref.at[:, mine, :], gath.at[here], xs.at[dx * nz], xr.at[dx * nz],
            {"x": lax.rem(x + dx, nx)},
        )

    def c_copy(dx, dz):
        at = slot(c, wrap(x - dx, nx), wrap(z - dz, nz))
        i = dx * nz + dz
        return remote(gath.at[at], gath.at[at], cs.at[i], cr.at[i], other)

    def c_own():
        return remote(keys_ref.at[:, mine, :], gath.at[here], cs.at[0], cr.at[0], other)

    def q_copy(i):
        peer = lax.rem(y + i, NY)
        return remote(q_ref.at[peer], qx.at[y], qs.at[i], qr.at[i], {"y": peer})

    def w_copy(i):
        peer = lax.rem(y + i, NY)
        return remote(w_ref.at[peer // 2], wx.at[y], ws.at[i], wr.at[i], {"y": peer})

    loop(1, nz, lambda k: z_copy(near(nz - k)).start())
    for dx in (2, 1, 3):
        x_own(dx).start()
    c_own().start()
    for i in (2, 1, 3):
        w_copy(i).start()
    for i in (2, 1, 3):
        q_copy(i).start()
    count_z.start(jnp.full((1, 128), live_here, jnp.int32).astype(F32))
    gath[here] = keys_ref[:, mine, :]
    wx[y] = w_ref[y // 2]

    def relay_z(k):
        dz = near(k)
        z_copy(dz).wait_recv()
        for dx in (2, 1, 3):
            x_copy(dx, dz).start()
        c_copy(0, dz).start()

    loop(1, nz, relay_z)
    count_x.start(count_z.finish())

    def invert(p):
        block = blocks_s[p]
        for tile in range(2):
            at = 2 * SLOTS
            for j in range(SLOTS):
                at = jnp.where(chosen_s[tile, j] == block, tile * SLOTS + j, at)
            inv[tile, p] = at

    loop(0, 4 * chips, invert)

    def relay_x(k):
        dz = near(k)
        for dx in (1, 3, 2):
            i = dx * nz + dz
            x_copy(dx, dz).wait_recv()
            c_copy(dx, dz).start()

    loop(0, nz, relay_x)
    count_c.start(count_x.finish())
    loop(0, chips, lambda i: c_copy(i // nz, lax.rem(i, nz)).wait_recv())

    for tile in range(2):
        for j in range(SLOTS):
            block = jnp.maximum(chosen_s[tile, j], 0)
            base = (block // 4) * 4
            pos = base
            for i in range(1, 4):
                pos = pos + jnp.where(blocks_s[base + i] == block, i, 0)
            device = pos // 2
            at = lax.rem(device, 2) * chips + device // 2
            sel[tile, j] = gath[at, lax.rem(pos, 2)]

    def k_copy(i):
        peer = lax.rem(y + i, NY)
        return remote(sel.at[peer // 2], kx.at[:, mine, :], ks.at[i], kr.at[i], {"y": peer})

    for i in (2, 1, 3):
        k_copy(i).start()
    kx[:, mine, :] = sel[y // 2]

    tile = y // 2
    half = lax.rem(y, 2) * ROWS
    for i in range(1, NY):
        w_copy(i).wait_recv()
    pick = (
        lax.broadcasted_iota(jnp.int32, (RG, BLOCK), 0) // HG + half
        == lax.broadcasted_iota(jnp.int32, (RG, BLOCK), 1)
    ).astype(F32).astype(BF16)
    head_lane = lax.rem(
        lax.broadcasted_iota(jnp.int32, (RG, BLOCK), 0), HG
    ) == lax.broadcasted_iota(jnp.int32, (RG, BLOCK), 1)
    ones = jnp.ones((BLOCK, BLOCK), BF16)
    for g in range(NY):
        wt = wx[g].astype(F32)
        wt = jnp.concatenate([wt, jnp.zeros((BLOCK - HG, BLOCK), F32)], axis=0).T.astype(BF16)
        row = jnp.dot(pick, wt, preferred_element_type=F32)
        row = jnp.where(head_lane, row, 0.0).astype(BF16)
        wb[g] = jnp.dot(row, ones, preferred_element_type=F32)
    own_q.wait()
    for i in range(1, NY):
        q_copy(i).wait_recv()
    for g in range(NY):
        for b in range(8):
            rows = slice(b * 128, (b + 1) * 128)
            wq = (qx[g, 8 * b : 8 * b + 8].reshape(128, DH).astype(F32) * wb[g, rows, :]).astype(BF16)
            qt[:, g * RG + b * 128 : g * RG + (b + 1) * 128] = wq.T
    count = count_c.finish() * float(BLOCK * BLOCK) - float(
        4 * chips * (BLOCK * BLOCK - BLOCK * (BLOCK + 1) // 2)
    )
    scale = (LOSS_SCALE * KEYS * SCORE_SCALE) / count
    for i in range(1, NY):
        k_copy(i).wait_recv()
    for j in range(SLOTS):
        kt[:, j * BLOCK : (j + 1) * BLOCK] = kx[j].T

    def forward(cc):
        cols = pl.ds(pl.multiple_of(cc * 256, 256), 256)
        keys_t = kt[:, cols]
        for tb in range(4):
            rows = slice(tb * 256, (tb + 1) * 256)
            acc = None
            for g in range(NY):
                qv = qx[g, 16 * tb : 16 * tb + 16].reshape(256, DH)
                d = jnp.dot(qv, keys_t, preferred_element_type=F32)
                dots[g * RG + tb * 256 : g * RG + (tb + 1) * 256, cols] = d.astype(BF16)
                wv = wb[g, rows, :]
                term = jnp.maximum(d, 0.0) * jnp.concatenate([wv, wv], axis=1)
                acc = term if acc is None else acc + term
            sc[tb * 16 : (tb + 1) * 16, cols] = (
                jnp.sum(acc.reshape(16, 16, 256), axis=1) * SCORE_SCALE
            )

    loop(0, KEYS // 256, forward)

    tcopy.wait()
    row = lax.broadcasted_iota(jnp.int32, (ROWS, BLOCK), 0) + half
    col = lax.broadcasted_iota(jnp.int32, (ROWS, BLOCK), 1)

    def live(j):
        on = jnp.full((ROWS, BLOCK), jnp.where(chosen_s[tile, j] >= 0, 1, 0), jnp.int32)
        if j == 0:
            on = jnp.where(col <= row, on, 0)
        return on > 0

    def part(j):
        return slice(j * BLOCK, (j + 1) * BLOCK)

    top = None
    tsum = None
    for j in range(SLOTS):
        s = jnp.where(live(j), sc[:, part(j)], -1e30)
        t = jnp.where(live(j), tgt[:, part(j)].astype(F32), 0.0)
        top = s if top is None else jnp.maximum(top, s)
        tsum = t if tsum is None else tsum + t
    row_max = jnp.max(top, axis=1, keepdims=True)
    row_t = 1.0 / jnp.sum(tsum, axis=1, keepdims=True)
    esum = None
    for j in range(SLOTS):
        e = jnp.where(live(j), jnp.exp(jnp.where(live(j), sc[:, part(j)] - row_max, 0.0)), 0.0)
        gs[:, part(j)] = e
        esum = e if esum is None else esum + e
    norm = jnp.sum(esum, axis=1, keepdims=True)
    row_n = 1.0 / norm
    lse = row_max + jnp.log(norm)
    kl = None
    for j in range(SLOTS):
        on = live(j)
        prob = jnp.where(on, tgt[:, part(j)].astype(F32) * row_t, 0.0)
        term = jnp.where(
            on, prob * (jnp.log(jnp.where(on, prob, 1.0)) - sc[:, part(j)] + lse), 0.0
        )
        kl = term if kl is None else kl + term
        gs[:, part(j)] = gs[:, part(j)] * row_n - prob
    kl_row = jnp.sum(kl, axis=0, keepdims=True)
    loss_y.start(jnp.broadcast_to(jnp.sum(kl_row, axis=1, keepdims=True), (1, 128)))

    def mask(i):
        for u in range(8):
            grad = jnp.broadcast_to(gs[pl.ds(i * 8 + u, 1), :], (HG, KEYS)).astype(BF16)
            for g in range(NY):
                at = pl.ds(pl.multiple_of(g * RG + i * 128 + u * HG, HG), HG)
                d = dots[at, :]
                dots[at, :] = jnp.where(d > 0, grad, jnp.zeros_like(grad))

    loop(0, ROWS // 8, mask)
    loss_z.start(loss_y.finish())

    def d_copy(i, part_of):
        peer = lax.rem(y + i, NY)
        some = pl.ds(part_of * (SLOTS // 2), SLOTS // 2)
        at = part_of * NY + i
        return remote(
            dks.at[peer, some], yrecv.at[y, some], ds_.at[at], dr.at[at], {"y": peer}
        )

    for part_of in range(2):
        def key_grad(cc):
            cols = pl.ds(pl.multiple_of(cc * 256, 256), 256)
            got = jnp.dot(qt[...], dots[:, cols], preferred_element_type=F32)
            for u in range(2):
                block = (got[:, u * 128 : (u + 1) * 128].T * scale).astype(BF16)
                for i in range(NY):
                    dks[i, cc * 2 + u] = block[i * QUARTER : (i + 1) * QUARTER]

        loop(part_of * 4, part_of * 4 + 4, key_grad)
        for i in (2, 1, 3):
            d_copy(i, part_of).start()
    loss_x.start(loss_z.finish())

    def qg_copy(i):
        peer = lax.rem(y + i, NY)
        return remote(qg.at[peer], oq.at[y], gs_.at[i], gr.at[i], {"y": peer})

    def wg_copy(i):
        peer = lax.rem(y + i, NY)
        return remote(wg.at[peer], wgr.at[y], vs.at[i], vr.at[i], {"y": peer})

    keys2 = kx[...].reshape(KEYS, DH)
    for i in (2, 1, 3, 0):
        g = lax.rem(y + i, NY)
        rows = pl.ds(pl.multiple_of(g * RG, RG), RG)
        a = jnp.dot(dots[rows, :], keys2, preferred_element_type=F32) * scale
        qg[g] = (a * wb[g]).astype(BF16).reshape(ROWS, HG, DH)
        s = jnp.sum(a.reshape(ROWS, HG, DH) * qx[g].astype(F32), axis=2).T
        nil = jnp.zeros((HG, ROWS), F32)
        wg[g] = jnp.where(
            half == 0, jnp.concatenate([s, nil], axis=1), jnp.concatenate([nil, s], axis=1)
        )
        if i > 0:
            wg_copy(i).start()
            qg_copy(i).start()
    own_o = pltpu.make_async_copy(qg.at[y], oq.at[y], osem)
    own_o.start()
    wgr[y] = wg[y]
    loss_c.start(loss_x.finish())

    yrecv[y] = dks[y]
    table[2 * SLOTS] = jnp.zeros((QUARTER, DH), F32)
    for part_of in range(2):
        for i in range(1, NY):
            d_copy(i, part_of).wait_recv()
    for t in range(2):
        def pair(j):
            table[t * SLOTS + j] = yrecv[2 * t, j].astype(F32) + yrecv[2 * t + 1, j].astype(F32)

        loop(0, SLOTS, pair)

    def dense(core, cx, dz, l):
        pos = slot(0, cx, lax.rem(z + dz, nz)) * 4 + core * 2 + l
        return table[inv[0, pos]] + table[inv[1, pos]]

    def e_copy(dz):
        return remote(dsend.at[dz], drecv.at[dz], es.at[dz], er.at[dz], other)

    def u_copy(dx, dz):
        to = lax.rem(x + dx, nx)
        i = dx * nz + dz
        return remote(pay.at[dz, to], xrecv.at[dx, dz], us.at[i], ur.at[i], {"x": to})

    def h_copy(dz):
        return remote(
            zsend.at[dz], zrecv.at[dz], hs.at[dz], hr.at[dz], {"z": lax.rem(z + dz, nz)}
        )

    def to_core(k):
        dz = near(nz - 1 - k)
        for cx in range(nx):
            for l in range(2):
                dsend[dz, cx, l] = dense(1 - c, cx, dz, l).astype(BF16)
        e_copy(dz).start()

    loop(0, nz, to_core)

    def to_x(k):
        dz = near(nz - 1 - k)
        e_copy(dz).wait_recv()
        for cx in range(nx):
            for l in range(2):
                v = dense(c, cx, dz, l) + drecv[dz, cx, l].astype(F32)
                pay[dz, cx, l] = v.astype(BF16)
        for dx in (2, 1, 3):
            u_copy(dx, dz).start()

    loop(0, nz, to_x)
    loss = loss_c.finish() * float(KEYS) / count
    ol[...] = jnp.broadcast_to(loss, (8, 128))

    def x_total(dz):
        total = pay[dz, x].astype(F32)
        for dx in (1, 3, 2):
            u_copy(dx, dz).wait_recv()
            total = total + xrecv[dx, dz].astype(F32)
        return total

    def to_z(k):
        dz = near(nz - 1 - k)
        zsend[dz] = x_total(dz).astype(BF16)
        h_copy(dz).start()

    loop(0, nz - 1, to_z)
    fin[...] = x_total(0)
    def add_z(k):
        dz = near(k)
        h_copy(dz).wait_recv()
        fin[...] += zrecv[dz].astype(F32)

    loop(1, nz, add_z)

    def f_copy(i):
        return remote(
            fin, ok.at[:, mine, :], fs.at[i], fr.at[i], {"y": lax.rem(y + i, NY)}
        )

    for i in (2, 1, 3):
        f_copy(i).start()
    ok[:, mine, :] = fin[...]

    for i in range(1, NY):
        wg_copy(i).wait_recv()
    ow[:, 0:128] = wgr[0] + wgr[1]
    ow[:, 128:256] = wgr[2] + wgr[3]
    own_o.wait()
    loop(1, nz, lambda dz: z_copy(dz).wait_send())
    c_own().wait_send()
    loop(1, chips, lambda i: c_copy(i // nz, lax.rem(i, nz)).wait_send())
    for dx in range(1, nx):
        loop(0, nz, lambda dz: (x_copy(dx, dz).wait_send(), u_copy(dx, dz).wait_send()))
    loop(0, nz, lambda dz: e_copy(dz).wait_send())
    loop(1, nz, lambda dz: h_copy(dz).wait_send())
    for i in range(1, NY):
        q_copy(i).wait_send()
        w_copy(i).wait_send()
        k_copy(i).wait_send()
        d_copy(i, 0).wait_send()
        d_copy(i, 1).wait_send()
        wg_copy(i).wait_send()
        qg_copy(i).wait()
        f_copy(i).wait()
    for r in rows_of:
        r.drain()


def finish_kernel(q_in, w_in, k_in, l_in, q_out, w_out, k_out, l_out):
    q_out[...] = q_in[...]
    w_out[...] = w_in[...]
    k_out[...] = k_in[...]
    l_out[0, 0] = l_in[0, 0]


VM = pl.BlockSpec(memory_space=pltpu.VMEM)
SM = pl.BlockSpec(memory_space=pltpu.SMEM)
ANY = pl.BlockSpec(memory_space=pl.ANY)


def shape(*dims_dtype):
    return jax.ShapeDtypeStruct(dims_dtype[:-1], dims_dtype[-1])


def local(nx, nz, queries, head_weights, keys, targets, chosen, tile_block):
    chips = nx * nz
    rows = NY * ROWS
    q4 = queries.reshape(NY, ROWS, HG, DH)
    w2 = jnp.stack([head_weights[:BLOCK].T, head_weights[BLOCK:].T])
    v = pltpu.VMEM
    scratch = [
        v((2 * chips, 2, QUARTER, DH), BF16),
        v((2, SLOTS, QUARTER, DH), BF16),
        v((NY, ROWS, HG, DH), BF16),
        v((NY, HG, BLOCK), BF16),
        v((SLOTS, BLOCK, DH), BF16),
        v((NY, RG, DH), F32),
        v((DH, NY * RG), BF16),
        v((DH, KEYS), BF16),
        v((NY * RG, KEYS), BF16),
        v((ROWS, KEYS), F32),
        v((ROWS, KEYS), F32),
        v((ROWS, KEYS), BF16),
        v((NY, ROWS, HG, DH), BF16),
        v((NY, HG, BLOCK), F32),
        v((NY, HG, BLOCK), F32),
        pltpu.SMEM((2, 4 * chips), jnp.int32),
        v((NY, SLOTS, QUARTER, DH), BF16),
        v((NY, SLOTS, QUARTER, DH), BF16),
        v((2 * SLOTS + 1, QUARTER, DH), F32),
        v((nz, nx, 2, QUARTER, DH), BF16),
        v((nz, nx, 2, QUARTER, DH), BF16),
        v((nz, nx, 2, QUARTER, DH), BF16),
        v((nx, nz, 2, QUARTER, DH), BF16),
        v((nz, 2, QUARTER, DH), BF16),
        v((nz, 2, QUARTER, DH), BF16),
        v((2, QUARTER, DH), F32),
        DMA, DMA, DMA,
    ]
    for n in (NY, NY, nz, chips, chips, NY, 2 * NY, NY, NY, nz, chips, nz, NY):
        scratch += [DMA((n,)), DMA((n,))]
    for n in (nz, nx, 2, NY, nz, nx, 2):
        scratch += row_sum_scratch(n)
    oq, ow, ok, ol = pl.pallas_call(
        functools.partial(kernel, nx, nz),
        out_shape=[
            shape(NY, ROWS, HG, DH, BF16),
            shape(HG, rows, F32),
            shape(2, BLOCK, DH, F32),
            shape(8, 128, F32),
        ],
        in_specs=[ANY, VM, VM, ANY, SM, SM],
        out_specs=[ANY, VM, VM, VM],
        scratch_shapes=scratch,
        compiler_params=pltpu.CompilerParams(
            collective_id=0, has_side_effects=True, vmem_limit_bytes=60 * 1024 * 1024
        ),
        name="step",
    )(q4, w2, keys.reshape(2, BLOCK, DH), targets.reshape(NY, ROWS, KEYS), chosen, tile_block)
    oq, ow, ok, ol = pl.pallas_call(
        finish_kernel,
        out_shape=[
            shape(NY, ROWS, HG, DH, BF16),
            shape(HG, rows, F32),
            shape(2, BLOCK, DH, F32),
            shape(1, 1, F32),
        ],
        in_specs=[VM, VM, VM, VM],
        out_specs=[VM, VM, VM, SM],
        name="finish",
    )(oq, ow, ok, ol)
    return oq.reshape(rows, HG, DH), ow.T, ok.reshape(rows, DH), ol[0, 0]


def solution(mesh):
    nx, nz = 4, mesh.shape["seq"] // 8
    torus = Mesh(mesh.devices.reshape(nx, nz, 2, mesh.shape["head"]), ("x", "z", "c", "y"))
    in_specs = (P(SEQ, "y", None), P(SEQ, "y"), P(SEQ, None), P(SEQ, None), P(SEQ, None), P())
    out_specs = (P(SEQ, "y", None), P(SEQ, "y"), P(SEQ, None), P())
    return jax.shard_map(
        functools.partial(local, nx, nz),
        mesh=torus, in_specs=in_specs, out_specs=out_specs, check_vma=False,
    )
```

time: 381 us -> 80.2 us (0.21)
  waiting for transfers between devices: 161 us -> 0 us
  Pallas kernels: 0 us -> 78.1 us
  blocking collectives: 62.1 us -> 0 us
  other arithmetic: 57.1 us -> 0.6 us
  matrix products: 37.2 us -> 0 us
  local copies, waits for them, and re-layouts: 27.4 us -> 0.71 us
  between operations: 18.7 us -> 0.64 us
  starting transfers between devices: 16 us -> 0 us
    all_to_all x3 -> x0, waiting for transfers between devices: 104 us -> none  [the longest x1 50.3 us: local(): lax.all_to_all(spread[tiles_here:].reshape(owner_count, CAP, BLOCK, key_w...]
    pallas_call x0 -> x2, Pallas kernels: none -> 78.1 us  [the longest x1 75.7 us: local(): pl.pallas_call(functools.partial(kernel, nx, nz), out_shape=[shape(NY, RO...]
    psum x1 -> x0, waiting for transfers between devices: 56.5 us -> none  [local(): score_part = lax.psum(partial_value, 'head')]
    psum x4 -> x0, blocking collectives: 40 us -> none  [over_axes(): value = lax.psum(value, axis)]
    dot_general x8 -> x0, matrix products: 37.2 us -> none  [the longest x4 19.5 us: dot_values(): jnp.einsum('qhd,kd->qhk', query_tile, key_tile.reshape(-1, key_width), pr...]
    all_to_all x1 -> x0, blocking collectives: 22.1 us -> none  [local(): lax.all_to_all(request, SEQ, split_axis=0, concat_axis=0, tiled=True)]
    reduce_sum x7 -> x0, other arithmetic: 22 us -> none  [the longest x2 14.9 us: backward(): jnp.sum(jnp.maximum(values, 0.0) * grad_tile[:, None, :], axis=2)]
    all_to_all x3 -> x0, starting transfers between devices: 16 us -> none  [the longest x1 6.84 us: local(): lax.all_to_all(spread[tiles_here:].reshape(owner_count, CAP, BLOCK, key_w...]
  transfers between devices with their start and end apart: 4 -> 0, of which waited for: 4 -> 0; matrix products, arithmetic and copies ran while one was open for 1% -> 0% of each run, Pallas kernels for 0% -> 0%
where the time goes in v2:
time: 80.2 us; the launch traced here: 80 us
  Pallas kernels  78.1 us (97%)
    pallas_call x1, Pallas kernels, local(): pl.pallas_call(functools.partial(kernel, nx, nz), out_shape=[shape(NY, RO...  75.7 us
    pallas_call x1, Pallas kernels, local(): pl.pallas_call(finish_kernel, out_shape=[shape(NY, ROWS, HG, DH, BF16), s...  2.33 us

profile of v2, /device:TPU:1, one launch (start us, length us, event | category | flops | bytes accessed | tf_op | source)
XLA Modules:
  0.0 80.0 jit_solution(3159285844287637076)
XLA Ops:
  0.6 0.7 slice_bitcast_fusion.1
  1.3 0.6 pad_maximum_fusion.w_ref
  1.9 75.7 %step.1 = (bf16[4,64,16,128]{3,2,1,0:T(8,128)(2,1)}, f32[16,256]{1,0:T(8,128)}, f32[2,128,128]{2,1,0:T(8,128)}, f32[8,128]{1,0:T(8,128)}) custom-call(bf16[4,64,16,128]{3,2,1,0:T(8,128)(2,1)} %bitcast.15, bf16[2,16,128]{2,1,0:T(8,128)(2,1)} %pad_maximum_fusion.w_ref, bf16[2,128,128]{2,1,0:T(8,128)(2,1)} %bitcast.17, bf16[4,64,2048]{2,1,0:T(8,128)(2,1)} %bitcast.16, ...), custom_call_target="tpu_custom_call" | custom-call | tf_op jit(solution)/shard_map/step/pallas_call | solution.py:534
  77.7 2.3 %finish.1 = (bf16[4,64,16,128]{3,2,1,0:T(8,128)(2,1)}, f32[16,256]{1,0:T(8,128)}, f32[2,128,128]{2,1,0:T(8,128)}, f32[1,1]{1,0:T(1,128)}) custom-call(bf16[4,64,16,128]{3,2,1,0:T(8,128)(2,1)} %get-tuple-element.12.q_in, f32[16,256]{1,0:T(8,128)} %get-tuple-element.13.w_in, f32[2,128,128]{2,1,0:T(8,128)} %get-tuple-element.14.k_in, ...), custom_call_target="tpu_custom_call" | custom-call | tf_op jit(solution)/shard_map/finish/pallas_call | solution.py:550

commit v3 on v2

--- a/solution.py
+++ b/solution.py
@@ -77,7 +77,7 @@
 def kernel(
     nx, nz, q_ref, w_ref, keys_ref, t_ref, chosen_s, blocks_s,
     oq, ow, ok, ol,
-    gath, sel, qx, wx, kx, wb, qt, kt, dots, sc, gs, tgt, qg, wg, wgr, inv,
+    gath, sel, qx, wx, kx, wb, qt, dots, sc, gs, traw, tgt, qg, wg, wgr, inv,
     dks, yrecv, table, dsend, drecv, pay, xrecv, zsend, zrecv, fin,
     tsem, lsem, osem, qs, qr, ws, wr, zs, zr, xs, xr, cs, cr, ks, kr,
     ds_, dr, gs_, gr, vs, vr, es, er, us, ur, hs, hr, fs, fr, *sums,
@@ -96,6 +96,10 @@
         odd = lax.rem(k, 2)
         return odd * ((k + 1) // 2) + (1 - odd) * lax.rem(nz - k // 2, nz)
 
+    def near4(k):
+        odd = lax.rem(k, 2)
+        return odd * ((k + 1) // 2) + (1 - odd) * lax.rem(NY - k // 2, NY)
+
     def wrap(v, n):
         return lax.rem(v + n, n)
 
@@ -104,7 +108,7 @@
         for i in range(1, size):
             peer = lax.rem(lax.axis_index(axis) + i, size)
             pl.semaphore_signal(barrier, inc=1, device_id={axis: peer}, device_id_type=MESH)
-    tcopy = pltpu.make_async_copy(t_ref.at[y], tgt, tsem)
+    tcopy = pltpu.make_async_copy(t_ref.at[y], traw, tsem)
     tcopy.start()
     own_q = pltpu.make_async_copy(q_ref.at[y], qx.at[y], lsem)
     own_q.start()
@@ -112,6 +116,27 @@
     for tile in range(2):
         for j in range(SLOTS):
             live_here = live_here + jnp.where(chosen_s[tile, j] >= 0, 1, 0)
+    def invert(p):
+        block = blocks_s[p]
+        for t in range(2):
+            at = 2 * SLOTS
+            for j in range(SLOTS):
+                at = jnp.where(chosen_s[t, j] == block, t * SLOTS + j, at)
+            inv[t, p] = at
+
+    loop(0, 2 * chips, invert)
+
+    tcopy.wait()
+    at_row = lax.broadcasted_iota(jnp.int32, (4 * BLOCK, BLOCK), 0)
+    at_col = lax.broadcasted_iota(jnp.int32, (4 * BLOCK, BLOCK), 1)
+    for q in range(NY):
+        source = (at_col // QUARTER) * BLOCK + q * QUARTER + lax.rem(at_col, QUARTER)
+        move = (at_row == source).astype(F32).astype(BF16)
+        for m in range(4):
+            got = jnp.dot(
+                traw[:, m * 512 : (m + 1) * 512], move, preferred_element_type=F32
+            )
+            tgt[:, q * 512 + m * 128 : q * 512 + (m + 1) * 128] = got.astype(BF16)
     pl.semaphore_wait(barrier, nz + nx + NY + 2 - 4)
 
     def slot(core, cx, cz):
@@ -150,7 +175,8 @@
 
     def w_copy(i):
         peer = lax.rem(y + i, NY)
-        return remote(w_ref.at[peer // 2], wx.at[y], ws.at[i], wr.at[i], {"y": peer})
+        lanes = pl.ds(pl.multiple_of((peer // 2) * BLOCK, BLOCK), BLOCK)
+        return remote(w_ref.at[:, lanes], wx.at[y], ws.at[i], wr.at[i], {"y": peer})
 
     loop(1, nz, lambda k: z_copy(near(nz - k)).start())
     for dx in (2, 1, 3):
@@ -162,7 +188,8 @@
         q_copy(i).start()
     count_z.start(jnp.full((1, 128), live_here, jnp.int32).astype(F32))
     gath[here] = keys_ref[:, mine, :]
-    wx[y] = w_ref[y // 2]
+    wx[y] = w_ref[:, pl.ds(pl.multiple_of((y // 2) * BLOCK, BLOCK), BLOCK)]
+    loop(2 * chips, 4 * chips, invert)
 
     def relay_z(k):
         dz = near(k)
@@ -173,46 +200,6 @@
 
     loop(1, nz, relay_z)
     count_x.start(count_z.finish())
-
-    def invert(p):
-        block = blocks_s[p]
-        for tile in range(2):
-            at = 2 * SLOTS
-            for j in range(SLOTS):
-                at = jnp.where(chosen_s[tile, j] == block, tile * SLOTS + j, at)
-            inv[tile, p] = at
-
-    loop(0, 4 * chips, invert)
-
-    def relay_x(k):
-        dz = near(k)
-        for dx in (1, 3, 2):
-            i = dx * nz + dz
-            x_copy(dx, dz).wait_recv()
-            c_copy(dx, dz).start()
-
-    loop(0, nz, relay_x)
-    count_c.start(count_x.finish())
-    loop(0, chips, lambda i: c_copy(i // nz, lax.rem(i, nz)).wait_recv())
-
-    for tile in range(2):
-        for j in range(SLOTS):
-            block = jnp.maximum(chosen_s[tile, j], 0)
-            base = (block // 4) * 4
-            pos = base
-            for i in range(1, 4):
-                pos = pos + jnp.where(blocks_s[base + i] == block, i, 0)
-            device = pos // 2
-            at = lax.rem(device, 2) * chips + device // 2
-            sel[tile, j] = gath[at, lax.rem(pos, 2)]
-
-    def k_copy(i):
-        peer = lax.rem(y + i, NY)
-        return remote(sel.at[peer // 2], kx.at[:, mine, :], ks.at[i], kr.at[i], {"y": peer})
-
-    for i in (2, 1, 3):
-        k_copy(i).start()
-    kx[:, mine, :] = sel[y // 2]
 
     tile = y // 2
     half = lax.rem(y, 2) * ROWS
@@ -232,6 +219,38 @@
         row = jnp.dot(pick, wt, preferred_element_type=F32)
         row = jnp.where(head_lane, row, 0.0).astype(BF16)
         wb[g] = jnp.dot(row, ones, preferred_element_type=F32)
+
+    def relay_x(k):
+        dz = near(k)
+        for dx in (1, 3, 2):
+            i = dx * nz + dz
+            x_copy(dx, dz).wait_recv()
+            c_copy(dx, dz).start()
+
+    loop(0, nz, relay_x)
+    count_c.start(count_x.finish())
+    loop(0, chips, lambda i: c_copy(i // nz, lax.rem(i, nz)).wait_recv())
+
+    for t in range(2):
+        for j in range(SLOTS):
+            block = jnp.maximum(chosen_s[t, j], 0)
+            base = (block // 4) * 4
+            pos = base
+            for i in range(1, 4):
+                pos = pos + jnp.where(blocks_s[base + i] == block, i, 0)
+            device = pos // 2
+            at = lax.rem(device, 2) * chips + device // 2
+            sel[t, j] = gath[at, lax.rem(pos, 2)]
+
+    def k_copy(i):
+        peer = lax.rem(y + i, NY)
+        return remote(sel.at[peer // 2], kx.at[y], ks.at[i], kr.at[i], {"y": peer})
+
+    for i in (2, 1, 3):
+        k_copy(i).start()
+    kx[y] = sel[tile]
+
+
     own_q.wait()
     for i in range(1, NY):
         q_copy(i).wait_recv()
@@ -244,14 +263,13 @@
         4 * chips * (BLOCK * BLOCK - BLOCK * (BLOCK + 1) // 2)
     )
     scale = (LOSS_SCALE * KEYS * SCORE_SCALE) / count
-    for i in range(1, NY):
-        k_copy(i).wait_recv()
-    for j in range(SLOTS):
-        kt[:, j * BLOCK : (j + 1) * BLOCK] = kx[j].T
-
-    def forward(cc):
-        cols = pl.ds(pl.multiple_of(cc * 256, 256), 256)
-        keys_t = kt[:, cols]
+
+    def forward(k, part_of):
+        at = wrap(y - near4(k), NY)
+        cols = pl.ds(pl.multiple_of(at * 512 + part_of * 256, 256), 256)
+        some = pl.ds(part_of * (SLOTS // 2), SLOTS // 2)
+        kv = kx[at, some].reshape(256, DH)
+        keys_t = jnp.concatenate([kv[:128].T, kv[128:].T], axis=1)
         for tb in range(4):
             rows = slice(tb * 256, (tb + 1) * 256)
             acc = None
@@ -266,16 +284,31 @@
                 jnp.sum(acc.reshape(16, 16, 256), axis=1) * SCORE_SCALE
             )
 
-    loop(0, KEYS // 256, forward)
-
-    tcopy.wait()
+    def quarter(k):
+        @pl.when(k > 0)
+        def _():
+            k_copy(near4(k)).wait_recv()
+
+        loop(0, 2, lambda part_of: forward(k, part_of))
+
+    loop(0, NY, quarter)
+
     row = lax.broadcasted_iota(jnp.int32, (ROWS, BLOCK), 0) + half
     col = lax.broadcasted_iota(jnp.int32, (ROWS, BLOCK), 1)
-
-    def live(j):
-        on = jnp.full((ROWS, BLOCK), jnp.where(chosen_s[tile, j] >= 0, 1, 0), jnp.int32)
-        if j == 0:
-            on = jnp.where(col <= row, on, 0)
+    group = col // QUARTER
+    chosen_on = []
+    for m in range(4):
+        on = jnp.zeros((ROWS, BLOCK), jnp.int32)
+        for u in range(4):
+            one = jnp.where(chosen_s[tile, 4 * m + u] >= 0, 1, 0)
+            on = jnp.where(group == u, jnp.full((ROWS, BLOCK), one, jnp.int32), on)
+        chosen_on.append(on)
+
+    def live(p):
+        q, m = p // 4, p % 4
+        on = chosen_on[m]
+        if m == 0:
+            on = jnp.where((group > 0) | (q * QUARTER + col <= row), on, 0)
         return on > 0
 
     def part(j):
@@ -310,38 +343,42 @@
     kl_row = jnp.sum(kl, axis=0, keepdims=True)
     loss_y.start(jnp.broadcast_to(jnp.sum(kl_row, axis=1, keepdims=True), (1, 128)))
 
-    def mask(i):
-        for u in range(8):
-            grad = jnp.broadcast_to(gs[pl.ds(i * 8 + u, 1), :], (HG, KEYS)).astype(BF16)
+    def d_copy(i):
+        peer = lax.rem(y + i, NY)
+        return remote(dks.at[peer], yrecv.at[y], ds_.at[i], dr.at[i], {"y": peer})
+
+    def key_grad(k, part_of):
+        at = lax.rem(y + near4(NY - 1 - k), NY)
+        cols = pl.ds(pl.multiple_of(at * 512 + part_of * 256, 256), 256)
+        got = None
+        for tb in range(4):
+            grad = jnp.concatenate(
+                [
+                    jnp.broadcast_to(gs[tb * 16 + u : tb * 16 + u + 1, cols], (HG, 256)).astype(BF16)
+                    for u in range(16)
+                ],
+                axis=0,
+            )
             for g in range(NY):
-                at = pl.ds(pl.multiple_of(g * RG + i * 128 + u * HG, HG), HG)
-                d = dots[at, :]
-                dots[at, :] = jnp.where(d > 0, grad, jnp.zeros_like(grad))
-
-    loop(0, ROWS // 8, mask)
+                rows = slice(g * RG + tb * 256, g * RG + (tb + 1) * 256)
+                d = dots[rows, cols]
+                d = jnp.where(d > 0, grad, jnp.zeros_like(grad))
+                dots[rows, cols] = d
+                term = jnp.dot(qt[:, rows], d, preferred_element_type=F32)
+                got = term if got is None else got + term
+        for u in range(2):
+            block = (got[:, u * 128 : (u + 1) * 128].T * scale).astype(BF16)
+            dks[at, pl.ds(part_of * 8 + u * 4, 4)] = block.reshape(4, QUARTER, DH)
+
+    def key_quarter(k):
+        loop(0, 2, lambda part_of: key_grad(k, part_of))
+
+        @pl.when(k < NY - 1)
+        def _():
+            d_copy(near4(NY - 1 - k)).start()
+
+    loop(0, NY, key_quarter)
     loss_z.start(loss_y.finish())
-
-    def d_copy(i, part_of):
-        peer = lax.rem(y + i, NY)
-        some = pl.ds(part_of * (SLOTS // 2), SLOTS // 2)
-        at = part_of * NY + i
-        return remote(
-            dks.at[peer, some], yrecv.at[y, some], ds_.at[at], dr.at[at], {"y": peer}
-        )
-
-    for part_of in range(2):
-        def key_grad(cc):
-            cols = pl.ds(pl.multiple_of(cc * 256, 256), 256)
-            got = jnp.dot(qt[...], dots[:, cols], preferred_element_type=F32)
-            for u in range(2):
-                block = (got[:, u * 128 : (u + 1) * 128].T * scale).astype(BF16)
-                for i in range(NY):
-                    dks[i, cc * 2 + u] = block[i * QUARTER : (i + 1) * QUARTER]
-
-        loop(part_of * 4, part_of * 4 + 4, key_grad)
-        for i in (2, 1, 3):
-            d_copy(i, part_of).start()
-    loss_x.start(loss_z.finish())
 
     def qg_copy(i):
         peer = lax.rem(y + i, NY)
@@ -351,30 +388,37 @@
         peer = lax.rem(y + i, NY)
         return remote(wg.at[peer], wgr.at[y], vs.at[i], vr.at[i], {"y": peer})
 
-    keys2 = kx[...].reshape(KEYS, DH)
-    for i in (2, 1, 3, 0):
+    def query_grad(i):
         g = lax.rem(y + i, NY)
         rows = pl.ds(pl.multiple_of(g * RG, RG), RG)
-        a = jnp.dot(dots[rows, :], keys2, preferred_element_type=F32) * scale
+        a = jnp.dot(dots[rows, :], kx[...].reshape(KEYS, DH), preferred_element_type=F32) * scale
         qg[g] = (a * wb[g]).astype(BF16).reshape(ROWS, HG, DH)
         s = jnp.sum(a.reshape(ROWS, HG, DH) * qx[g].astype(F32), axis=2).T
         nil = jnp.zeros((HG, ROWS), F32)
         wg[g] = jnp.where(
             half == 0, jnp.concatenate([s, nil], axis=1), jnp.concatenate([nil, s], axis=1)
         )
-        if i > 0:
-            wg_copy(i).start()
-            qg_copy(i).start()
-    own_o = pltpu.make_async_copy(qg.at[y], oq.at[y], osem)
-    own_o.start()
-    wgr[y] = wg[y]
-    loss_c.start(loss_x.finish())
+
+    for i in (2, 1, 3):
+        query_grad(i)
+        wg_copy(i).start()
+        qg_copy(i).start()
+    loss_x.start(loss_z.finish())
+    loop(1, nz, lambda dz: z_copy(dz).wait_send())
+    c_own().wait_send()
+    loop(1, chips, lambda i: c_copy(i // nz, lax.rem(i, nz)).wait_send())
+    loop(nz, chips, lambda i: x_copy(i // nz, lax.rem(i, nz)).wait_send())
+    for i in range(1, NY):
+        q_copy(i).wait_send()
+        w_copy(i).wait_send()
+        k_copy(i).wait_send()
+    for r in rows_of[:3]:
+        r.drain()
 
     yrecv[y] = dks[y]
     table[2 * SLOTS] = jnp.zeros((QUARTER, DH), F32)
-    for part_of in range(2):
-        for i in range(1, NY):
-            d_copy(i, part_of).wait_recv()
+    for i in range(1, NY):
+        d_copy(i).wait_recv()
     for t in range(2):
         def pair(j):
             table[t * SLOTS + j] = yrecv[2 * t, j].astype(F32) + yrecv[2 * t + 1, j].astype(F32)
@@ -406,6 +450,11 @@
         e_copy(dz).start()
 
     loop(0, nz, to_core)
+    query_grad(0)
+    own_o = pltpu.make_async_copy(qg.at[y], oq.at[y], osem)
+    own_o.start()
+    wgr[y] = wg[y]
+    loss_c.start(loss_x.finish())
 
     def to_x(k):
         dz = near(nz - 1 - k)
@@ -456,31 +505,36 @@
     ow[:, 0:128] = wgr[0] + wgr[1]
     ow[:, 128:256] = wgr[2] + wgr[3]
     own_o.wait()
-    loop(1, nz, lambda dz: z_copy(dz).wait_send())
-    c_own().wait_send()
-    loop(1, chips, lambda i: c_copy(i // nz, lax.rem(i, nz)).wait_send())
-    for dx in range(1, nx):
-        loop(0, nz, lambda dz: (x_copy(dx, dz).wait_send(), u_copy(dx, dz).wait_send()))
+    loop(nz, chips, lambda i: u_copy(i // nz, lax.rem(i, nz)).wait_send())
     loop(0, nz, lambda dz: e_copy(dz).wait_send())
     loop(1, nz, lambda dz: h_copy(dz).wait_send())
+    for r in rows_of[3:]:
+        r.drain()
     for i in range(1, NY):
-        q_copy(i).wait_send()
-        w_copy(i).wait_send()
-        k_copy(i).wait_send()
-        d_copy(i, 0).wait_send()
-        d_copy(i, 1).wait_send()
+        d_copy(i).wait_send()
         wg_copy(i).wait_send()
         qg_copy(i).wait()
+    for i in range(1, NY):
         f_copy(i).wait()
-    for r in rows_of:
-        r.drain()
-
-
-def finish_kernel(q_in, w_in, k_in, l_in, q_out, w_out, k_out, l_out):
-    q_out[...] = q_in[...]
+
+
+def finish_kernel(q_in, w_in, k_in, l_in, q_out, w_out, k_out, l_out, hold, isem, osem):
+    def take(g):
+        return pltpu.make_async_copy(q_in.at[g], hold.at[g], isem.at[g])
+
+    def put(g):
+        return pltpu.make_async_copy(hold.at[g], q_out.at[g], osem.at[g])
+
+    for g in range(NY):
+        take(g).start()
     w_out[...] = w_in[...]
     k_out[...] = k_in[...]
     l_out[0, 0] = l_in[0, 0]
+    for g in range(NY):
+        take(g).wait()
+        put(g).start()
+    for g in range(NY):
+        put(g).wait()
 
 
 VM = pl.BlockSpec(memory_space=pltpu.VMEM)
@@ -496,20 +550,19 @@
     chips = nx * nz
     rows = NY * ROWS
     q4 = queries.reshape(NY, ROWS, HG, DH)
-    w2 = jnp.stack([head_weights[:BLOCK].T, head_weights[BLOCK:].T])
     v = pltpu.VMEM
     scratch = [
         v((2 * chips, 2, QUARTER, DH), BF16),
         v((2, SLOTS, QUARTER, DH), BF16),
         v((NY, ROWS, HG, DH), BF16),
         v((NY, HG, BLOCK), BF16),
-        v((SLOTS, BLOCK, DH), BF16),
+        v((NY, SLOTS, QUARTER, DH), BF16),
         v((NY, RG, DH), F32),
         v((DH, NY * RG), BF16),
-        v((DH, KEYS), BF16),
         v((NY * RG, KEYS), BF16),
         v((ROWS, KEYS), F32),
         v((ROWS, KEYS), F32),
+        v((ROWS, KEYS), BF16),
         v((ROWS, KEYS), BF16),
         v((NY, ROWS, HG, DH), BF16),
         v((NY, HG, BLOCK), F32),
@@ -527,7 +580,7 @@
         v((2, QUARTER, DH), F32),
         DMA, DMA, DMA,
     ]
-    for n in (NY, NY, nz, chips, chips, NY, 2 * NY, NY, NY, nz, chips, nz, NY):
+    for n in (NY, NY, nz, chips, chips, NY, NY, NY, NY, nz, chips, nz, NY):
         scratch += [DMA((n,)), DMA((n,))]
     for n in (nz, nx, 2, NY, nz, nx, 2):
         scratch += row_sum_scratch(n)
@@ -546,7 +599,7 @@
             collective_id=0, has_side_effects=True, vmem_limit_bytes=60 * 1024 * 1024
         ),
         name="step",
-    )(q4, w2, keys.reshape(2, BLOCK, DH), targets.reshape(NY, ROWS, KEYS), chosen, tile_block)
+    )(q4, head_weights.T, keys.reshape(2, BLOCK, DH), targets.reshape(NY, ROWS, KEYS), chosen, tile_block)
     oq, ow, ok, ol = pl.pallas_call(
         finish_kernel,
         out_shape=[
@@ -555,8 +608,9 @@
             shape(2, BLOCK, DH, F32),
             shape(1, 1, F32),
         ],
-        in_specs=[VM, VM, VM, VM],
-        out_specs=[VM, VM, VM, SM],
+        in_specs=[ANY, VM, VM, VM],
+        out_specs=[ANY, VM, VM, SM],
+        scratch_shapes=[v((NY, ROWS, HG, DH), BF16), DMA((NY,)), DMA((NY,))],
         name="finish",
     )(oq, ow, ok, ol)
     return oq.reshape(rows, HG, DH), ow.T, ok.reshape(rows, DH), ol[0, 0]

time: 80.2 us -> 77.3 us (0.964); the launches traced: 80 us -> 76.3 us
  Pallas kernels: 78.1 us -> 75.7 us
    pallas_call x1, Pallas kernels: 75.7 us -> 72.1 us  [local(): pl.pallas_call(functools.partial(kernel, nx, nz), out_shape=[shape(NY, RO...]
    pallas_call x1, Pallas kernels: 2.33 us -> 3.56 us  [local(): pl.pallas_call(finish_kernel, out_shape=[shape(NY, ROWS, HG, DH, BF16), s...]
where the time goes in v3:
time: 77.3 us; the launch traced here: 76.3 us
  Pallas kernels  75.7 us (98%)
    pallas_call x1, Pallas kernels, local(): pl.pallas_call(functools.partial(kernel, nx, nz), out_shape=[shape(NY, RO...  72.1 us
    pallas_call x1, Pallas kernels, local(): pl.pallas_call(finish_kernel, out_shape=[shape(NY, ROWS, HG, DH, BF16), s...  3.56 us

profile of v3, /device:TPU:1, one launch (start us, length us, event | category | flops | bytes accessed | tf_op | source)
XLA Modules:
  0.0 76.3 jit_solution(16692530722965533267)
XLA Ops:
  0.6 72.1 %step.1 = (bf16[4,64,16,128]{3,2,1,0:T(8,128)(2,1)}, f32[16,256]{1,0:T(8,128)}, f32[2,128,128]{2,1,0:T(8,128)}, f32[8,128]{1,0:T(8,128)}) custom-call(bf16[4,64,16,128]{3,2,1,0:T(8,128)(2,1)} %bitcast.8, bf16[16,256]{1,0:T(8,128)(2,1)} %bitcast.11, bf16[2,128,128]{2,1,0:T(8,128)(2,1)} %bitcast.10, bf16[4,64,2048]{2,1,0:T(8,128)(2,1)} %bitcast.9, ...), custom_call_target="tpu_custom_call" | custom-call | tf_op jit(solution)/shard_map/step/pallas_call | solution.py:587
  72.7 3.6 %finish.1 = (bf16[4,64,16,128]{3,2,1,0:T(8,128)(2,1)}, f32[16,256]{1,0:T(8,128)}, f32[2,128,128]{2,1,0:T(8,128)}, f32[1,1]{1,0:T(1,128)}) custom-call(bf16[4,64,16,128]{3,2,1,0:T(8,128)(2,1)} %get-tuple-element.12.q_in, f32[16,256]{1,0:T(8,128)} %get-tuple-element.13.w_in, f32[2,128,128]{2,1,0:T(8,128)} %get-tuple-element.14.k_in, ...), custom_call_target="tpu_custom_call" | custom-call | tf_op jit(solution)/shard_map/finish/pallas_call | solution.py:603

commit v4 on v3

--- a/solution.py
+++ b/solution.py
@@ -75,9 +75,9 @@
 
 
 def kernel(
-    nx, nz, q_ref, w_ref, keys_ref, t_ref, chosen_s, blocks_s,
+    nx, nz, q_ref, w_hbm, keys_hbm, t_ref, chosen_s, blocks_s,
     oq, ow, ok, ol,
-    gath, sel, qx, wx, kx, wb, qt, dots, sc, gs, traw, tgt, qg, wg, wgr, inv,
+    w_ref, keys_ref, ow_v, ol_v, fin_b, isem, rsem, gath, sel, qx, wx, kx, wb, qt, dots, sc, gs, traw, tgt, qg, wg, wgr, inv,
     dks, yrecv, table, dsend, drecv, pay, xrecv, zsend, zrecv, fin,
     tsem, lsem, osem, qs, qr, ws, wr, zs, zr, xs, xr, cs, cr, ks, kr,
     ds_, dr, gs_, gr, vs, vr, es, er, us, ur, hs, hr, fs, fr, *sums,
@@ -85,6 +85,8 @@
     chips = nx * nz
     x, z, c, y = (lax.axis_index(a) for a in ("x", "z", "c", "y"))
     other = {"c": 1 - c}
+    tile = y // 2
+    half = lax.rem(y, 2) * ROWS
     mine = pl.ds(pl.multiple_of(y * QUARTER, QUARTER), QUARTER)
     sizes = [("z", nz), ("x", nx), ("c", 2), ("y", NY), ("z", nz), ("x", nx), ("c", 2)]
     rows_of = [
@@ -108,14 +110,24 @@
         for i in range(1, size):
             peer = lax.rem(lax.axis_index(axis) + i, size)
             pl.semaphore_signal(barrier, inc=1, device_id={axis: peer}, device_id_type=MESH)
+    inputs = [
+        pltpu.make_async_copy(src, dst, isem.at[i])
+        for i, (src, dst) in enumerate(
+            ((keys_hbm, keys_ref), (w_hbm, w_ref))
+        )
+    ]
+    for copy in inputs:
+        copy.start()
     tcopy = pltpu.make_async_copy(t_ref.at[y], traw, tsem)
     tcopy.start()
     own_q = pltpu.make_async_copy(q_ref.at[y], qx.at[y], lsem)
     own_q.start()
+    for copy in inputs:
+        copy.wait()
     live_here = 0
-    for tile in range(2):
+    for t in range(2):
         for j in range(SLOTS):
-            live_here = live_here + jnp.where(chosen_s[tile, j] >= 0, 1, 0)
+            live_here = live_here + jnp.where(chosen_s[t, j] >= 0, 1, 0)
     def invert(p):
         block = blocks_s[p]
         for t in range(2):
@@ -201,8 +213,36 @@
     loop(1, nz, relay_z)
     count_x.start(count_z.finish())
 
-    tile = y // 2
-    half = lax.rem(y, 2) * ROWS
+    def relay_x(k):
+        dz = near(k)
+        for dx in (1, 3, 2):
+            i = dx * nz + dz
+            x_copy(dx, dz).wait_recv()
+            c_copy(dx, dz).start()
+
+    loop(0, nz, relay_x)
+    count_c.start(count_x.finish())
+    loop(0, chips, lambda i: c_copy(i // nz, lax.rem(i, nz)).wait_recv())
+
+    for t in range(2):
+        for j in range(SLOTS):
+            block = jnp.maximum(chosen_s[t, j], 0)
+            base = (block // 4) * 4
+            pos = base
+            for i in range(1, 4):
+                pos = pos + jnp.where(blocks_s[base + i] == block, i, 0)
+            device = pos // 2
+            at = lax.rem(device, 2) * chips + device // 2
+            sel[t, j] = gath[at, lax.rem(pos, 2)]
+
+    def k_copy(i):
+        peer = lax.rem(y + i, NY)
+        return remote(sel.at[peer // 2], kx.at[y], ks.at[i], kr.at[i], {"y": peer})
+
+    for i in (2, 1, 3):
+        k_copy(i).start()
+    kx[y] = sel[tile]
+
     for i in range(1, NY):
         w_copy(i).wait_recv()
     pick = (
@@ -219,36 +259,6 @@
         row = jnp.dot(pick, wt, preferred_element_type=F32)
         row = jnp.where(head_lane, row, 0.0).astype(BF16)
         wb[g] = jnp.dot(row, ones, preferred_element_type=F32)
-
-    def relay_x(k):
-        dz = near(k)
-        for dx in (1, 3, 2):
-            i = dx * nz + dz
-            x_copy(dx, dz).wait_recv()
-            c_copy(dx, dz).start()
-
-    loop(0, nz, relay_x)
-    count_c.start(count_x.finish())
-    loop(0, chips, lambda i: c_copy(i // nz, lax.rem(i, nz)).wait_recv())
-
-    for t in range(2):
-        for j in range(SLOTS):
-            block = jnp.maximum(chosen_s[t, j], 0)
-            base = (block // 4) * 4
-            pos = base
-            for i in range(1, 4):
-                pos = pos + jnp.where(blocks_s[base + i] == block, i, 0)
-            device = pos // 2
-            at = lax.rem(device, 2) * chips + device // 2
-            sel[t, j] = gath[at, lax.rem(pos, 2)]
-
-    def k_copy(i):
-        peer = lax.rem(y + i, NY)
-        return remote(sel.at[peer // 2], kx.at[y], ks.at[i], kr.at[i], {"y": peer})
-
-    for i in (2, 1, 3):
-        k_copy(i).start()
-    kx[y] = sel[tile]
 
 
     own_q.wait()
@@ -401,8 +411,6 @@
 
     for i in (2, 1, 3):
         query_grad(i)
-        wg_copy(i).start()
-        qg_copy(i).start()
     loss_x.start(loss_z.finish())
     loop(1, nz, lambda dz: z_copy(dz).wait_send())
     c_own().wait_send()
@@ -419,6 +427,9 @@
     table[2 * SLOTS] = jnp.zeros((QUARTER, DH), F32)
     for i in range(1, NY):
         d_copy(i).wait_recv()
+    for i in (2, 1, 3):
+        wg_copy(i).start()
+        qg_copy(i).start()
     for t in range(2):
         def pair(j):
             table[t * SLOTS + j] = yrecv[2 * t, j].astype(F32) + yrecv[2 * t + 1, j].astype(F32)
@@ -468,7 +479,7 @@
 
     loop(0, nz, to_x)
     loss = loss_c.finish() * float(KEYS) / count
-    ol[...] = jnp.broadcast_to(loss, (8, 128))
+    ol_v[...] = jnp.broadcast_to(loss, (8, 128))
 
     def x_total(dz):
         total = pay[dz, x].astype(F32)
@@ -493,17 +504,23 @@
 
     def f_copy(i):
         return remote(
-            fin, ok.at[:, mine, :], fs.at[i], fr.at[i], {"y": lax.rem(y + i, NY)}
-        )
-
+            fin_b, ok.at[:, mine, :], fs.at[i], fr.at[i], {"y": lax.rem(y + i, NY)}
+        )
+
+    fin_b[...] = fin[...].astype(BF16)
     for i in (2, 1, 3):
         f_copy(i).start()
-    ok[:, mine, :] = fin[...]
 
     for i in range(1, NY):
         wg_copy(i).wait_recv()
-    ow[:, 0:128] = wgr[0] + wgr[1]
-    ow[:, 128:256] = wgr[2] + wgr[3]
+    ow_v[:, 0:128] = wgr[0] + wgr[1]
+    ow_v[:, 128:256] = wgr[2] + wgr[3]
+    results = [
+        pltpu.make_async_copy(src, dst, rsem.at[i])
+        for i, (src, dst) in enumerate(((fin_b, ok.at[:, mine, :]), (ol_v, ol), (ow_v, ow)))
+    ]
+    for copy in results:
+        copy.start()
     own_o.wait()
     loop(nz, chips, lambda i: u_copy(i // nz, lax.rem(i, nz)).wait_send())
     loop(0, nz, lambda dz: e_copy(dz).wait_send())
@@ -514,27 +531,17 @@
         d_copy(i).wait_send()
         wg_copy(i).wait_send()
         qg_copy(i).wait()
+    for copy in results:
+        copy.wait()
     for i in range(1, NY):
         f_copy(i).wait()
 
 
-def finish_kernel(q_in, w_in, k_in, l_in, q_out, w_out, k_out, l_out, hold, isem, osem):
-    def take(g):
-        return pltpu.make_async_copy(q_in.at[g], hold.at[g], isem.at[g])
-
-    def put(g):
-        return pltpu.make_async_copy(hold.at[g], q_out.at[g], osem.at[g])
-
-    for g in range(NY):
-        take(g).start()
+def finish_kernel(q_in, w_in, k_in, l_in, q_out, w_out, k_out, l_out):
+    q_out[...] = q_in[...]
     w_out[...] = w_in[...]
-    k_out[...] = k_in[...]
+    k_out[...] = k_in[...].astype(F32)
     l_out[0, 0] = l_in[0, 0]
-    for g in range(NY):
-        take(g).wait()
-        put(g).start()
-    for g in range(NY):
-        put(g).wait()
 
 
 VM = pl.BlockSpec(memory_space=pltpu.VMEM)
@@ -552,6 +559,8 @@
     q4 = queries.reshape(NY, ROWS, HG, DH)
     v = pltpu.VMEM
     scratch = [
+        v((HG, rows), BF16), v((2, BLOCK, DH), BF16),
+        v((HG, rows), F32), v((8, 128), F32), v((2, QUARTER, DH), BF16), DMA((2,)), DMA((3,)),
         v((2 * chips, 2, QUARTER, DH), BF16),
         v((2, SLOTS, QUARTER, DH), BF16),
         v((NY, ROWS, HG, DH), BF16),
@@ -589,11 +598,11 @@
         out_shape=[
             shape(NY, ROWS, HG, DH, BF16),
             shape(HG, rows, F32),
-            shape(2, BLOCK, DH, F32),
+            shape(2, BLOCK, DH, BF16),
             shape(8, 128, F32),
         ],
-        in_specs=[ANY, VM, VM, ANY, SM, SM],
-        out_specs=[ANY, VM, VM, VM],
+        in_specs=[ANY, ANY, ANY, ANY, SM, SM],
+        out_specs=[ANY] * 4,
         scratch_shapes=scratch,
         compiler_params=pltpu.CompilerParams(
             collective_id=0, has_side_effects=True, vmem_limit_bytes=60 * 1024 * 1024
@@ -608,9 +617,8 @@
             shape(2, BLOCK, DH, F32),
             shape(1, 1, F32),
         ],
-        in_specs=[ANY, VM, VM, VM],
-        out_specs=[ANY, VM, VM, SM],
-        scratch_shapes=[v((NY, ROWS, HG, DH), BF16), DMA((NY,)), DMA((NY,))],
+        in_specs=[VM, VM, VM, VM],
+        out_specs=[VM, VM, VM, SM],
         name="finish",
     )(oq, ow, ok, ol)
     return oq.reshape(rows, HG, DH), ow.T, ok.reshape(rows, DH), ol[0, 0]

time: 77.3 us -> 72.2 us (0.934)
  Pallas kernels: 75.7 us -> 71 us
    pallas_call x1, Pallas kernels: 72.1 us -> 68.7 us  [local(): pl.pallas_call(functools.partial(kernel, nx, nz), out_shape=[shape(NY, RO...]
    pallas_call x1, Pallas kernels: 3.56 us -> 2.33 us  [local(): pl.pallas_call(finish_kernel, out_shape=[shape(NY, ROWS, HG, DH, BF16), s...]
where the time goes in v4:
time: 72.2 us; the launch traced here: 71.6 us
  Pallas kernels  71 us (98%)
    pallas_call x1, Pallas kernels, local(): pl.pallas_call(functools.partial(kernel, nx, nz), out_shape=[shape(NY, RO...  68.7 us
    pallas_call x1, Pallas kernels, local(): pl.pallas_call(finish_kernel, out_shape=[shape(NY, ROWS, HG, DH, BF16), s...  2.33 us

profile of v4, /device:TPU:1, one launch (start us, length us, event | category | flops | bytes accessed | tf_op | source)
XLA Modules:
  0.0 71.6 jit_solution(18209586564637560934)
XLA Ops:
  0.6 68.7 %step.1 = (bf16[4,64,16,128]{3,2,1,0:T(8,128)(2,1)}, f32[16,256]{1,0:T(8,128)}, bf16[2,128,128]{2,1,0:T(8,128)(2,1)}, f32[8,128]{1,0:T(8,128)}) custom-call(bf16[4,64,16,128]{3,2,1,0:T(8,128)(2,1)} %bitcast.8, bf16[16,256]{1,0:T(8,128)(2,1)} %bitcast.11, bf16[2,128,128]{2,1,0:T(8,128)(2,1)} %bitcast.10, bf16[4,64,2048]{2,1,0:T(8,128)(2,1)} %bitcast.9, ...), custom_call_target="tpu_custom_call" | custom-call | tf_op jit(solution)/shard_map/step/pallas_call | solution.py:596
  69.3 2.3 %finish.1 = (bf16[4,64,16,128]{3,2,1,0:T(8,128)(2,1)}, f32[16,256]{1,0:T(8,128)}, f32[2,128,128]{2,1,0:T(8,128)}, f32[1,1]{1,0:T(1,128)}) custom-call(bf16[4,64,16,128]{3,2,1,0:T(8,128)(2,1)} %get-tuple-element.12.q_in, f32[16,256]{1,0:T(8,128)} %get-tuple-element.13.w_in, bf16[2,128,128]{2,1,0:T(8,128)(2,1)} %get-tuple-element.14.k_in, ...), custom_call_target="tpu_custom_call" | custom-call | tf_op jit(solution)/shard_map/finish/pallas_call | solution.py:612

commit v5 on v4

--- a/solution.py
+++ b/solution.py
@@ -239,7 +239,7 @@
         peer = lax.rem(y + i, NY)
         return remote(sel.at[peer // 2], kx.at[y], ks.at[i], kr.at[i], {"y": peer})
 
-    for i in (2, 1, 3):
+    for i in (1, 3, 2):
         k_copy(i).start()
     kx[y] = sel[tile]
 
@@ -409,7 +409,7 @@
             half == 0, jnp.concatenate([s, nil], axis=1), jnp.concatenate([nil, s], axis=1)
         )
 
-    for i in (2, 1, 3):
+    for i in (2, 1, 3, 0):
         query_grad(i)
     loss_x.start(loss_z.finish())
     loop(1, nz, lambda dz: z_copy(dz).wait_send())
@@ -461,7 +461,6 @@
         e_copy(dz).start()
 
     loop(0, nz, to_core)
-    query_grad(0)
     own_o = pltpu.make_async_copy(qg.at[y], oq.at[y], osem)
     own_o.start()
     wgr[y] = wg[y]

time: 72.2 us -> 70.4 us (0.975)
  Pallas kernels: 71 us -> 69.2 us
    pallas_call x1, Pallas kernels: 68.7 us -> 66.9 us  [local(): pl.pallas_call(functools.partial(kernel, nx, nz), out_shape=[shape(NY, RO...]
where the time goes in v5:
time: 70.4 us; the launch traced here: 69.9 us
  Pallas kernels  69.2 us (98%)
    pallas_call x1, Pallas kernels, local(): pl.pallas_call(functools.partial(kernel, nx, nz), out_shape=[shape(NY, RO...  66.9 us
    pallas_call x1, Pallas kernels, local(): pl.pallas_call(finish_kernel, out_shape=[shape(NY, ROWS, HG, DH, BF16), s...  2.33 us

profile of v5, /device:TPU:1, one launch (start us, length us, event | category | flops | bytes accessed | tf_op | source)
XLA Modules:
  0.0 69.9 jit_solution(3571965135589683138)
XLA Ops:
  0.6 66.9 %step.1 = (bf16[4,64,16,128]{3,2,1,0:T(8,128)(2,1)}, f32[16,256]{1,0:T(8,128)}, bf16[2,128,128]{2,1,0:T(8,128)(2,1)}, f32[8,128]{1,0:T(8,128)}) custom-call(bf16[4,64,16,128]{3,2,1,0:T(8,128)(2,1)} %bitcast.8, bf16[16,256]{1,0:T(8,128)(2,1)} %bitcast.11, bf16[2,128,128]{2,1,0:T(8,128)(2,1)} %bitcast.10, bf16[4,64,2048]{2,1,0:T(8,128)(2,1)} %bitcast.9, ...), custom_call_target="tpu_custom_call" | custom-call | tf_op jit(solution)/shard_map/step/pallas_call | solution.py:595
  67.5 2.3 %finish.1 = (bf16[4,64,16,128]{3,2,1,0:T(8,128)(2,1)}, f32[16,256]{1,0:T(8,128)}, f32[2,128,128]{2,1,0:T(8,128)}, f32[1,1]{1,0:T(1,128)}) custom-call(bf16[4,64,16,128]{3,2,1,0:T(8,128)(2,1)} %get-tuple-element.12.q_in, f32[16,256]{1,0:T(8,128)} %get-tuple-element.13.w_in, bf16[2,128,128]{2,1,0:T(8,128)(2,1)} %get-tuple-element.14.k_in, ...), custom_call_target="tpu_custom_call" | custom-call | tf_op jit(solution)/shard_map/finish/pallas_call | solution.py:611

commit v6 on v5

--- a/solution.py
+++ b/solution.py
@@ -154,7 +154,10 @@
     def slot(core, cx, cz):
         return core * chips + cx * nz + cz
 
-    here = slot(c, x, z)
+    def held(core, cx, cz):
+        return core * chips + cz * nx + cx
+
+    here = held(c, x, z)
 
     def z_copy(dz):
         return remote(
@@ -163,7 +166,7 @@
         )
 
     def x_copy(dx, dz):
-        at = slot(c, x, wrap(z - dz, nz))
+        at = held(c, x, wrap(z - dz, nz))
         i = dx * nz + dz
         return remote(gath.at[at], gath.at[at], xs.at[i], xr.at[i], {"x": lax.rem(x + dx, nx)})
 
@@ -173,13 +176,9 @@
             {"x": lax.rem(x + dx, nx)},
         )
 
-    def c_copy(dx, dz):
-        at = slot(c, wrap(x - dx, nx), wrap(z - dz, nz))
-        i = dx * nz + dz
-        return remote(gath.at[at], gath.at[at], cs.at[i], cr.at[i], other)
-
-    def c_own():
-        return remote(keys_ref.at[:, mine, :], gath.at[here], cs.at[0], cr.at[0], other)
+    def c_copy(dz):
+        some = pl.ds(held(c, 0, wrap(z - dz, nz)), nx)
+        return remote(gath.at[some], gath.at[some], cs.at[dz], cr.at[dz], other)
 
     def q_copy(i):
         peer = lax.rem(y + i, NY)
@@ -193,7 +192,6 @@
     loop(1, nz, lambda k: z_copy(near(nz - k)).start())
     for dx in (2, 1, 3):
         x_own(dx).start()
-    c_own().start()
     for i in (2, 1, 3):
         w_copy(i).start()
     for i in (2, 1, 3):
@@ -208,7 +206,6 @@
         z_copy(dz).wait_recv()
         for dx in (2, 1, 3):
             x_copy(dx, dz).start()
-        c_copy(0, dz).start()
 
     loop(1, nz, relay_z)
     count_x.start(count_z.finish())
@@ -216,13 +213,12 @@
     def relay_x(k):
         dz = near(k)
         for dx in (1, 3, 2):
-            i = dx * nz + dz
             x_copy(dx, dz).wait_recv()
-            c_copy(dx, dz).start()
+        c_copy(dz).start()
 
     loop(0, nz, relay_x)
     count_c.start(count_x.finish())
-    loop(0, chips, lambda i: c_copy(i // nz, lax.rem(i, nz)).wait_recv())
+    loop(0, nz, lambda dz: c_copy(dz).wait_recv())
 
     for t in range(2):
         for j in range(SLOTS):
@@ -232,7 +228,7 @@
             for i in range(1, 4):
                 pos = pos + jnp.where(blocks_s[base + i] == block, i, 0)
             device = pos // 2
-            at = lax.rem(device, 2) * chips + device // 2
+            at = held(lax.rem(device, 2), device // (2 * nz), lax.rem(device // 2, nz))
             sel[t, j] = gath[at, lax.rem(pos, 2)]
 
     def k_copy(i):
@@ -413,8 +409,7 @@
         query_grad(i)
     loss_x.start(loss_z.finish())
     loop(1, nz, lambda dz: z_copy(dz).wait_send())
-    c_own().wait_send()
-    loop(1, chips, lambda i: c_copy(i // nz, lax.rem(i, nz)).wait_send())
+    loop(0, nz, lambda dz: c_copy(dz).wait_send())
     loop(nz, chips, lambda i: x_copy(i // nz, lax.rem(i, nz)).wait_send())
     for i in range(1, NY):
         q_copy(i).wait_send()
@@ -588,7 +583,7 @@
         v((2, QUARTER, DH), F32),
         DMA, DMA, DMA,
     ]
-    for n in (NY, NY, nz, chips, chips, NY, NY, NY, NY, nz, chips, nz, NY):
+    for n in (NY, NY, nz, chips, nz, NY, NY, NY, NY, nz, chips, nz, NY):
         scratch += [DMA((n,)), DMA((n,))]
     for n in (nz, nx, 2, NY, nz, nx, 2):
         scratch += row_sum_scratch(n)

time: 70.4 us -> 68.2 us (0.969)
  Pallas kernels: 69.2 us -> 67 us
    pallas_call x1, Pallas kernels: 66.9 us -> 64.7 us  [local(): pl.pallas_call(functools.partial(kernel, nx, nz), out_shape=[shape(NY, RO...]
where the time goes in v6:
time: 68.2 us; the launch traced here: 67.7 us
  Pallas kernels  67 us (98%)
    pallas_call x1, Pallas kernels, local(): pl.pallas_call(functools.partial(kernel, nx, nz), out_shape=[shape(NY, RO...  64.7 us
    pallas_call x1, Pallas kernels, local(): pl.pallas_call(finish_kernel, out_shape=[shape(NY, ROWS, HG, DH, BF16), s...  2.33 us

profile of v6, /device:TPU:1, one launch (start us, length us, event | category | flops | bytes accessed | tf_op | source)
XLA Modules:
  0.0 67.7 jit_solution(7985900853825780829)
XLA Ops:
  0.6 64.7 %step.1 = (bf16[4,64,16,128]{3,2,1,0:T(8,128)(2,1)}, f32[16,256]{1,0:T(8,128)}, bf16[2,128,128]{2,1,0:T(8,128)(2,1)}, f32[8,128]{1,0:T(8,128)}) custom-call(bf16[4,64,16,128]{3,2,1,0:T(8,128)(2,1)} %bitcast.8, bf16[16,256]{1,0:T(8,128)(2,1)} %bitcast.11, bf16[2,128,128]{2,1,0:T(8,128)(2,1)} %bitcast.10, bf16[4,64,2048]{2,1,0:T(8,128)(2,1)} %bitcast.9, ...), custom_call_target="tpu_custom_call" | custom-call | tf_op jit(solution)/shard_map/step/pallas_call | solution.py:590
  65.3 2.3 %finish.1 = (bf16[4,64,16,128]{3,2,1,0:T(8,128)(2,1)}, f32[16,256]{1,0:T(8,128)}, f32[2,128,128]{2,1,0:T(8,128)}, f32[1,1]{1,0:T(1,128)}) custom-call(bf16[4,64,16,128]{3,2,1,0:T(8,128)(2,1)} %get-tuple-element.12.q_in, f32[16,256]{1,0:T(8,128)} %get-tuple-element.13.w_in, bf16[2,128,128]{2,1,0:T(8,128)(2,1)} %get-tuple-element.14.k_in, ...), custom_call_target="tpu_custom_call" | custom-call | tf_op jit(solution)/shard_map/finish/pallas_call | solution.py:606
